TPU v7x, 32 devices: a whole 2x2x4 slice. The times are simulated.
32 devices in a mesh: dp: 2 (over x), cols: 4 (over z), rows: 4 (over y, core).
Axes of the slice: x: 2, y: 2, z: 4, core: 2. Of those that a mesh axis runs over, the one named last changes fastest.
Arguments:
- frames: bfloat16 [24, 2, 192, 128, 16], P(None, 'dp', 'rows', 'cols'), parts along dimension 1
- w_in: bfloat16 [3, 3, 16, 512], replicated
- w_rec: bfloat16 [3, 3, 128, 512], replicated
- gate_bias: float32 [512], replicated
- h_init: bfloat16 [2, 192, 128, 128], P('dp', 'rows', 'cols'), parts along dimension 0
- c_init: float32 [2, 192, 128, 128], P('dp', 'rows', 'cols'), parts along dimension 0
Outputs:
- output 1: bfloat16 [24, 2, 192, 128, 128], P(None, 'dp', 'rows', 'cols'), parts along dimension 1
- output 2: float32 [2, 192, 128, 128], P('dp', 'rows', 'cols'), parts along dimension 0
There are 2 independent parts. A program takes and returns all parts, laid end to end along the dimension named above; an argument that names none is the same for every part.
All inputs are finite; a program needn't handle non-finite values.
Results may differ from a plain program's by a relative error of at most 0.00438231.
Values are sent between devices in bfloat16 or wider.
A program may use at most 1 GiB of HBM per device.

v0:
```python
import jax
import jax.numpy as jnp
from jax import lax
from jax.sharding import PartitionSpec as P, NamedSharding

CONV_DIMS = ("NHWC", "HWIO", "NHWC")


def conv_valid(operand, kernel):
    return lax.conv_general_dilated(operand, kernel, (1, 1), "VALID", dimension_numbers=CONV_DIMS, preferred_element_type=jnp.float32)


def cell_update(gate_pre, c_prev):
    gate_i, gate_f, gate_o, gate_g = jnp.split(gate_pre, 4, axis=-1)
    c_next = jax.nn.sigmoid(gate_f) * c_prev + jax.nn.sigmoid(gate_i) * jnp.tanh(gate_g)
    h_next = (jax.nn.sigmoid(gate_o) * jnp.tanh(c_next)).astype(jnp.bfloat16)
    return h_next, c_next


def edge_exchange(tile_in, axis_name, axis_size, axis_dim, width):
    length = tile_in.shape[axis_dim]
    low_part = lax.slice_in_dim(tile_in, 0, width, axis=axis_dim)
    high_part = lax.slice_in_dim(tile_in, length - width, length, axis=axis_dim)
    if axis_size == 1:
        from_prev = jnp.zeros_like(high_part)
        from_next = jnp.zeros_like(low_part)
    else:
        forward = [(source, source + 1) for source in range(axis_size - 1)]
        backward = [(source + 1, source) for source in range(axis_size - 1)]
        from_prev = lax.ppermute(high_part, axis_name, forward)
        from_next = lax.ppermute(low_part, axis_name, backward)
    return jnp.concatenate([from_prev, tile_in, from_next], axis=axis_dim)


def add_halo(tile_in, width, n_rows, n_cols):
    row_dim = tile_in.ndim - 3
    tall_tile = edge_exchange(tile_in, "rows", n_rows, row_dim, width)
    return edge_exchange(tall_tile, "cols", n_cols, row_dim + 1, width)


def solution(mesh):
    n_rows = mesh.shape["rows"]
    n_cols = mesh.shape["cols"]
    seq_spec = P(None, "dp", "rows", "cols", None)
    state_spec = P("dp", "rows", "cols", None)

    def local_run(frames, w_in, w_rec, gate_bias, h_init, c_init):
        frames_ext = add_halo(frames, 1, n_rows, n_cols)

        def time_step(carry_in, frame_ext):
            h_prev, c_prev = carry_in
            h_ext = add_halo(h_prev, 1, n_rows, n_cols)
            gate_pre = conv_valid(frame_ext, w_in) + conv_valid(h_ext, w_rec) + gate_bias
            h_next, c_next = cell_update(gate_pre, c_prev)
            return (h_next, c_next), h_next

        (h_last, c_last), hidden_seq = lax.scan(time_step, (h_init, c_init), frames_ext)
        return hidden_seq, c_last

    return jax.shard_map(local_run, mesh=mesh, in_specs=(seq_spec, P(), P(), P(), state_spec, state_spec), out_specs=(seq_spec, state_spec), check_vma=False)
```

profile of v0, /device:TPU:0, one launch (start us, length us, event | category | flops | bytes accessed | tf_op | source)
XLA Modules:
  0.0 599.0 jit_solution(2272977977786392830)
XLA Ops:
  0.6 6.0 %fusion.31 = (bf16[24,1,1,32,16]{2,4,3,1,0:T(8,128)(2,1)}, bf16[24,1,1,32,16]{2,4,3,1,0:T(8,128)(2,1)S(1)}) fusion(bf16[24,1,48,32,16]{2,4,3,1,0:T(8,128)(2,1)} %param.8), kind=kLoop, calls=%fused_computation.49 | loop fusion | bytes 98304 | tf_op jit(solution)/shard_map/slice | solution.py:23
  27.8 4.9 collective-permute-start.6
  39.1 6.0 %pad_maximum_fusion.3 = bf16[24,1,50,34,16]{2,4,3,1,0:T(8,128)(2,1)} fusion(bf16[24,1,50,1,16]{2,4,3,1,0:T(8,128)(2,1)} %collective-permute-done.7, bf16[24,1,1,32,16]{2,4,3,1,0:T(8,128)(2,1)} %copy.28, bf16[24,1,48,32,16]{2,4,3,1,0:T(8,128)(2,1)S(1)} %copy-done, bf16[24,1,1,32,16]{2,4,3,1,0:T(8,128)(2,1)} %copy.27, ...), kind=kLoop, calls=%fused_computation.44 | loop fusion | flops 6528000 | bytes 2611200 | tf_op jit(solution)/shard_map/concatenate | solution.py:32
  45.2 551.6 %while.14 = (s32[]{:T(128)}, bf16[1,48,32,128]{3,1,2,0:T(8,128)(2,1)S(1)}, f32[1,48,32,128]{3,1,2,0:T(8,128)}, bf16[24,1,48,32,128]{4,3,2,1,0:T(8,128)(2,1)}, bf...) while((s32[]{:T(128)}, ...), condition=%wide.region_1.2_spmd, body=%wide.region_0.1_spmd.sunk | while | flops 2559887872 | bytes 47861176 | solution.py:57
  52.6 4.7 collective-permute-start.3
  91.0 5.2 collective-permute-start.1
  114.3 5.0 collective-permute-start.1
  121.6 4.5 collective-permute-start.3
  137.3 5.0 collective-permute-start.1
  144.6 4.5 collective-permute-start.3
  160.4 5.0 collective-permute-start.1
  167.7 4.5 collective-permute-start.3
  183.4 4.9 collective-permute-start.1
  190.7 4.5 collective-permute-start.3
  206.5 5.0 collective-permute-start.1
  229.5 4.9 collective-permute-start.1
  252.5 5.0 collective-permute-start.1
  275.6 5.0 collective-permute-start.1
  298.6 5.0 collective-permute-start.1
  321.6 5.0 collective-permute-start.1
  344.7 4.9 collective-permute-start.1
  367.7 5.0 collective-permute-start.1
  390.8 5.0 collective-permute-start.1
  398.0 4.5 collective-permute-start.3
  413.8 5.0 collective-permute-start.1
  436.9 4.9 collective-permute-start.1
  460.0 4.9 collective-permute-start.1
  483.0 5.0 collective-permute-start.1
  506.1 4.9 collective-permute-start.1
  529.1 5.0 collective-permute-start.1
  552.2 4.9 collective-permute-start.1
  575.2 4.9 collective-permute-start.1
  (834 shorter events, 439.9 us)
Async XLA Ops:
  10.9 7.0 %collective-permute-start.4 = (bf16[24,1,1,32,16]{3,4,2,1,0:T(8,128)(2,1)S(1)}, bf16[24,1,1,32,16]{3,4,2,1,0:T(8,128)(2,1)S(1)}, u32[]{:S(2)}, u32[]{:S(2)}) collective-permute-start(bf16[24,1,1,32,16]{3,4,2,1,0:T(8,128)(2,1)S(1)} %copy.35), channel_id=1, source_target_pairs={{0,1},{1,2},{2,3},{4,5},{5,6},{6,7},{8,9},{9,10},{10,11},{12,13},{... | collective-permute-start | bytes 73736 | tf_op jit(solution)/shard_map/ppermute | solution.py:30
  27.8 10.0 %collective-permute-start.6 = (bf16[24,1,50,1,16]{2,4,3,1,0:T(8,128)(2,1)}, bf16[24,1,50,1,16]{2,4,3,1,0:T(8,128)(2,1)}, u32[]{:S(2)}, u32[]{:S(2)}) collective-permute-start(bf16[24,1,50,1,16]{2,4,3,1,0:T(8,128)(2,1)} %get-tuple-element.92), channel_id=1, source_target_pairs={{0,4},{4,8},{8,12},{1,5},{5,9},{9,13},{2,6},{6,10},{10,14},{3,7},{... | collective-permute-start | bytes 115208 | tf_op jit(solution)/shard_map/ppermute | solution.py:30
  32.6 6.5 %collective-permute-start.7 = (bf16[24,1,50,1,16]{2,4,3,1,0:T(8,128)(2,1)}, bf16[24,1,50,1,16]{2,4,3,1,0:T(8,128)(2,1)}, u32[]{:S(2)}, u32[]{:S(2)}) collective-permute-start(bf16[24,1,50,1,16]{2,4,3,1,0:T(8,128)(2,1)} %get-tuple-element.93), channel_id=1, source_target_pairs={{4,0},{8,4},{12,8},{5,1},{9,5},{13,9},{6,2},{10,6},{14,10},{7,3},{... | collective-permute-start | bytes 115208 | tf_op jit(solution)/shard_map/ppermute | solution.py:31
  51.3 6.6 %collective-permute-start.2 = (bf16[1,50,1,128]{3,1,2,0:T(8,128)(2,1)S(1)}, bf16[1,50,1,128]{3,1,2,0:T(8,128)(2,1)S(1)}, u32[]{:S(2)}, u32[]{:S(2)}) collective-permute-start(bf16[1,50,1,128]{3,1,2,0:T(8,128)(2,1)S(1)} %get-tuple-element.156), channel_id=1, source_target_pairs={{4,0},{8,4},{12,8},{5,1},{9,5},{13,9},{6,2},{10,6},{14,10},{7,3},{... | collective-permute-start | bytes 38408 | tf_op jit(solution)/shard_map/while/body/eval_jaxpr/ppermute | solution.py:31
  67.0 6.8 %collective-permute-start = (bf16[1,1,32,128]{3,1,2,0:T(2,128)(2,1)S(1)}, bf16[1,1,32,128]{3,1,2,0:T(2,128)(2,1)S(1)}, u32[]{:S(2)}, u32[]{:S(2)}) collective-permute-start(bf16[1,1,32,128]{3,1,2,0:T(2,128)(2,1)S(1)} %get-tuple-element.154), channel_id=1, source_target_pairs={{1,0},{2,1},{3,2},{5,4},{6,5},{7,6},{9,8},{10,9},{11,10},{13,12},{... | collective-permute-start | bytes 24584 | tf_op jit(solution)/shard_map/while/body/eval_jaxpr/ppermute | solution.py:31
  89.5 7.7 %collective-permute-start = (bf16[1,1,32,128]{3,1,2,0:T(2,128)(2,1)S(1)}, bf16[1,1,32,128]{3,1,2,0:T(2,128)(2,1)S(1)}, u32[]{:S(2)}, u32[]{:S(2)}) collective-permute-start(bf16[1,1,32,128]{3,1,2,0:T(2,128)(2,1)S(1)} %get-tuple-element.154), channel_id=1, source_target_pairs={{1,0},{2,1},{3,2},{5,4},{6,5},{7,6},{9,8},{10,9},{11,10},{13,12},{... | collective-permute-start | bytes 24584 | tf_op jit(solution)/shard_map/while/body/eval_jaxpr/ppermute | solution.py:31
  112.9 7.4 %collective-permute-start = (bf16[1,1,32,128]{3,1,2,0:T(2,128)(2,1)S(1)}, bf16[1,1,32,128]{3,1,2,0:T(2,128)(2,1)S(1)}, u32[]{:S(2)}, u32[]{:S(2)}) collective-permute-start(bf16[1,1,32,128]{3,1,2,0:T(2,128)(2,1)S(1)} %get-tuple-element.154), channel_id=1, source_target_pairs={{1,0},{2,1},{3,2},{5,4},{6,5},{7,6},{9,8},{10,9},{11,10},{13,12},{... | collective-permute-start | bytes 24584 | tf_op jit(solution)/shard_map/while/body/eval_jaxpr/ppermute | solution.py:31
  120.3 6.4 %collective-permute-start.2 = (bf16[1,50,1,128]{3,1,2,0:T(8,128)(2,1)S(1)}, bf16[1,50,1,128]{3,1,2,0:T(8,128)(2,1)S(1)}, u32[]{:S(2)}, u32[]{:S(2)}) collective-permute-start(bf16[1,50,1,128]{3,1,2,0:T(8,128)(2,1)S(1)} %get-tuple-element.156), channel_id=1, source_target_pairs={{4,0},{8,4},{12,8},{5,1},{9,5},{13,9},{6,2},{10,6},{14,10},{7,3},{... | collective-permute-start | bytes 38408 | tf_op jit(solution)/shard_map/while/body/eval_jaxpr/ppermute | solution.py:31
  135.9 7.4 %collective-permute-start = (bf16[1,1,32,128]{3,1,2,0:T(2,128)(2,1)S(1)}, bf16[1,1,32,128]{3,1,2,0:T(2,128)(2,1)S(1)}, u32[]{:S(2)}, u32[]{:S(2)}) collective-permute-start(bf16[1,1,32,128]{3,1,2,0:T(2,128)(2,1)S(1)} %get-tuple-element.154), channel_id=1, source_target_pairs={{1,0},{2,1},{3,2},{5,4},{6,5},{7,6},{9,8},{10,9},{11,10},{13,12},{... | collective-permute-start | bytes 24584 | tf_op jit(solution)/shard_map/while/body/eval_jaxpr/ppermute | solution.py:31
  143.3 6.4 %collective-permute-start.2 = (bf16[1,50,1,128]{3,1,2,0:T(8,128)(2,1)S(1)}, bf16[1,50,1,128]{3,1,2,0:T(8,128)(2,1)S(1)}, u32[]{:S(2)}, u32[]{:S(2)}) collective-permute-start(bf16[1,50,1,128]{3,1,2,0:T(8,128)(2,1)S(1)} %get-tuple-element.156), channel_id=1, source_target_pairs={{4,0},{8,4},{12,8},{5,1},{9,5},{13,9},{6,2},{10,6},{14,10},{7,3},{... | collective-permute-start | bytes 38408 | tf_op jit(solution)/shard_map/while/body/eval_jaxpr/ppermute | solution.py:31
  158.9 7.4 %collective-permute-start = (bf16[1,1,32,128]{3,1,2,0:T(2,128)(2,1)S(1)}, bf16[1,1,32,128]{3,1,2,0:T(2,128)(2,1)S(1)}, u32[]{:S(2)}, u32[]{:S(2)}) collective-permute-start(bf16[1,1,32,128]{3,1,2,0:T(2,128)(2,1)S(1)} %get-tuple-element.154), channel_id=1, source_target_pairs={{1,0},{2,1},{3,2},{5,4},{6,5},{7,6},{9,8},{10,9},{11,10},{13,12},{... | collective-permute-start | bytes 24584 | tf_op jit(solution)/shard_map/while/body/eval_jaxpr/ppermute | solution.py:31
  166.4 6.4 %collective-permute-start.2 = (bf16[1,50,1,128]{3,1,2,0:T(8,128)(2,1)S(1)}, bf16[1,50,1,128]{3,1,2,0:T(8,128)(2,1)S(1)}, u32[]{:S(2)}, u32[]{:S(2)}) collective-permute-start(bf16[1,50,1,128]{3,1,2,0:T(8,128)(2,1)S(1)} %get-tuple-element.156), channel_id=1, source_target_pairs={{4,0},{8,4},{12,8},{5,1},{9,5},{13,9},{6,2},{10,6},{14,10},{7,3},{... | collective-permute-start | bytes 38408 | tf_op jit(solution)/shard_map/while/body/eval_jaxpr/ppermute | solution.py:31
  182.0 7.4 %collective-permute-start = (bf16[1,1,32,128]{3,1,2,0:T(2,128)(2,1)S(1)}, bf16[1,1,32,128]{3,1,2,0:T(2,128)(2,1)S(1)}, u32[]{:S(2)}, u32[]{:S(2)}) collective-permute-start(bf16[1,1,32,128]{3,1,2,0:T(2,128)(2,1)S(1)} %get-tuple-element.154), channel_id=1, source_target_pairs={{1,0},{2,1},{3,2},{5,4},{6,5},{7,6},{9,8},{10,9},{11,10},{13,12},{... | collective-permute-start | bytes 24584 | tf_op jit(solution)/shard_map/while/body/eval_jaxpr/ppermute | solution.py:31
  205.0 7.4 %collective-permute-start = (bf16[1,1,32,128]{3,1,2,0:T(2,128)(2,1)S(1)}, bf16[1,1,32,128]{3,1,2,0:T(2,128)(2,1)S(1)}, u32[]{:S(2)}, u32[]{:S(2)}) collective-permute-start(bf16[1,1,32,128]{3,1,2,0:T(2,128)(2,1)S(1)} %get-tuple-element.154), channel_id=1, source_target_pairs={{1,0},{2,1},{3,2},{5,4},{6,5},{7,6},{9,8},{10,9},{11,10},{13,12},{... | collective-permute-start | bytes 24584 | tf_op jit(solution)/shard_map/while/body/eval_jaxpr/ppermute | solution.py:31
  212.4 6.4 %collective-permute-start.2 = (bf16[1,50,1,128]{3,1,2,0:T(8,128)(2,1)S(1)}, bf16[1,50,1,128]{3,1,2,0:T(8,128)(2,1)S(1)}, u32[]{:S(2)}, u32[]{:S(2)}) collective-permute-start(bf16[1,50,1,128]{3,1,2,0:T(8,128)(2,1)S(1)} %get-tuple-element.156), channel_id=1, source_target_pairs={{4,0},{8,4},{12,8},{5,1},{9,5},{13,9},{6,2},{10,6},{14,10},{7,3},{... | collective-permute-start | bytes 38408 | tf_op jit(solution)/shard_map/while/body/eval_jaxpr/ppermute | solution.py:31
  228.1 7.4 %collective-permute-start = (bf16[1,1,32,128]{3,1,2,0:T(2,128)(2,1)S(1)}, bf16[1,1,32,128]{3,1,2,0:T(2,128)(2,1)S(1)}, u32[]{:S(2)}, u32[]{:S(2)}) collective-permute-start(bf16[1,1,32,128]{3,1,2,0:T(2,128)(2,1)S(1)} %get-tuple-element.154), channel_id=1, source_target_pairs={{1,0},{2,1},{3,2},{5,4},{6,5},{7,6},{9,8},{10,9},{11,10},{13,12},{... | collective-permute-start | bytes 24584 | tf_op jit(solution)/shard_map/while/body/eval_jaxpr/ppermute | solution.py:31
  235.5 6.4 %collective-permute-start.2 = (bf16[1,50,1,128]{3,1,2,0:T(8,128)(2,1)S(1)}, bf16[1,50,1,128]{3,1,2,0:T(8,128)(2,1)S(1)}, u32[]{:S(2)}, u32[]{:S(2)}) collective-permute-start(bf16[1,50,1,128]{3,1,2,0:T(8,128)(2,1)S(1)} %get-tuple-element.156), channel_id=1, source_target_pairs={{4,0},{8,4},{12,8},{5,1},{9,5},{13,9},{6,2},{10,6},{14,10},{7,3},{... | collective-permute-start | bytes 38408 | tf_op jit(solution)/shard_map/while/body/eval_jaxpr/ppermute | solution.py:31
  251.1 7.4 %collective-permute-start = (bf16[1,1,32,128]{3,1,2,0:T(2,128)(2,1)S(1)}, bf16[1,1,32,128]{3,1,2,0:T(2,128)(2,1)S(1)}, u32[]{:S(2)}, u32[]{:S(2)}) collective-permute-start(bf16[1,1,32,128]{3,1,2,0:T(2,128)(2,1)S(1)} %get-tuple-element.154), channel_id=1, source_target_pairs={{1,0},{2,1},{3,2},{5,4},{6,5},{7,6},{9,8},{10,9},{11,10},{13,12},{... | collective-permute-start | bytes 24584 | tf_op jit(solution)/shard_map/while/body/eval_jaxpr/ppermute | solution.py:31
  274.1 7.4 %collective-permute-start = (bf16[1,1,32,128]{3,1,2,0:T(2,128)(2,1)S(1)}, bf16[1,1,32,128]{3,1,2,0:T(2,128)(2,1)S(1)}, u32[]{:S(2)}, u32[]{:S(2)}) collective-permute-start(bf16[1,1,32,128]{3,1,2,0:T(2,128)(2,1)S(1)} %get-tuple-element.154), channel_id=1, source_target_pairs={{1,0},{2,1},{3,2},{5,4},{6,5},{7,6},{9,8},{10,9},{11,10},{13,12},{... | collective-permute-start | bytes 24584 | tf_op jit(solution)/shard_map/while/body/eval_jaxpr/ppermute | solution.py:31
  297.2 7.4 %collective-permute-start = (bf16[1,1,32,128]{3,1,2,0:T(2,128)(2,1)S(1)}, bf16[1,1,32,128]{3,1,2,0:T(2,128)(2,1)S(1)}, u32[]{:S(2)}, u32[]{:S(2)}) collective-permute-start(bf16[1,1,32,128]{3,1,2,0:T(2,128)(2,1)S(1)} %get-tuple-element.154), channel_id=1, source_target_pairs={{1,0},{2,1},{3,2},{5,4},{6,5},{7,6},{9,8},{10,9},{11,10},{13,12},{... | collective-permute-start | bytes 24584 | tf_op jit(solution)/shard_map/while/body/eval_jaxpr/ppermute | solution.py:31
  320.2 7.4 %collective-permute-start = (bf16[1,1,32,128]{3,1,2,0:T(2,128)(2,1)S(1)}, bf16[1,1,32,128]{3,1,2,0:T(2,128)(2,1)S(1)}, u32[]{:S(2)}, u32[]{:S(2)}) collective-permute-start(bf16[1,1,32,128]{3,1,2,0:T(2,128)(2,1)S(1)} %get-tuple-element.154), channel_id=1, source_target_pairs={{1,0},{2,1},{3,2},{5,4},{6,5},{7,6},{9,8},{10,9},{11,10},{13,12},{... | collective-permute-start | bytes 24584 | tf_op jit(solution)/shard_map/while/body/eval_jaxpr/ppermute | solution.py:31
  343.2 7.4 %collective-permute-start = (bf16[1,1,32,128]{3,1,2,0:T(2,128)(2,1)S(1)}, bf16[1,1,32,128]{3,1,2,0:T(2,128)(2,1)S(1)}, u32[]{:S(2)}, u32[]{:S(2)}) collective-permute-start(bf16[1,1,32,128]{3,1,2,0:T(2,128)(2,1)S(1)} %get-tuple-element.154), channel_id=1, source_target_pairs={{1,0},{2,1},{3,2},{5,4},{6,5},{7,6},{9,8},{10,9},{11,10},{13,12},{... | collective-permute-start | bytes 24584 | tf_op jit(solution)/shard_map/while/body/eval_jaxpr/ppermute | solution.py:31
  366.3 7.4 %collective-permute-start = (bf16[1,1,32,128]{3,1,2,0:T(2,128)(2,1)S(1)}, bf16[1,1,32,128]{3,1,2,0:T(2,128)(2,1)S(1)}, u32[]{:S(2)}, u32[]{:S(2)}) collective-permute-start(bf16[1,1,32,128]{3,1,2,0:T(2,128)(2,1)S(1)} %get-tuple-element.154), channel_id=1, source_target_pairs={{1,0},{2,1},{3,2},{5,4},{6,5},{7,6},{9,8},{10,9},{11,10},{13,12},{... | collective-permute-start | bytes 24584 | tf_op jit(solution)/shard_map/while/body/eval_jaxpr/ppermute | solution.py:31
  389.3 7.4 %collective-permute-start = (bf16[1,1,32,128]{3,1,2,0:T(2,128)(2,1)S(1)}, bf16[1,1,32,128]{3,1,2,0:T(2,128)(2,1)S(1)}, u32[]{:S(2)}, u32[]{:S(2)}) collective-permute-start(bf16[1,1,32,128]{3,1,2,0:T(2,128)(2,1)S(1)} %get-tuple-element.154), channel_id=1, source_target_pairs={{1,0},{2,1},{3,2},{5,4},{6,5},{7,6},{9,8},{10,9},{11,10},{13,12},{... | collective-permute-start | bytes 24584 | tf_op jit(solution)/shard_map/while/body/eval_jaxpr/ppermute | solution.py:31
  412.4 7.4 %collective-permute-start = (bf16[1,1,32,128]{3,1,2,0:T(2,128)(2,1)S(1)}, bf16[1,1,32,128]{3,1,2,0:T(2,128)(2,1)S(1)}, u32[]{:S(2)}, u32[]{:S(2)}) collective-permute-start(bf16[1,1,32,128]{3,1,2,0:T(2,128)(2,1)S(1)} %get-tuple-element.154), channel_id=1, source_target_pairs={{1,0},{2,1},{3,2},{5,4},{6,5},{7,6},{9,8},{10,9},{11,10},{13,12},{... | collective-permute-start | bytes 24584 | tf_op jit(solution)/shard_map/while/body/eval_jaxpr/ppermute | solution.py:31
  435.5 7.4 %collective-permute-start = (bf16[1,1,32,128]{3,1,2,0:T(2,128)(2,1)S(1)}, bf16[1,1,32,128]{3,1,2,0:T(2,128)(2,1)S(1)}, u32[]{:S(2)}, u32[]{:S(2)}) collective-permute-start(bf16[1,1,32,128]{3,1,2,0:T(2,128)(2,1)S(1)} %get-tuple-element.154), channel_id=1, source_target_pairs={{1,0},{2,1},{3,2},{5,4},{6,5},{7,6},{9,8},{10,9},{11,10},{13,12},{... | collective-permute-start | bytes 24584 | tf_op jit(solution)/shard_map/while/body/eval_jaxpr/ppermute | solution.py:31
  458.5 7.4 %collective-permute-start = (bf16[1,1,32,128]{3,1,2,0:T(2,128)(2,1)S(1)}, bf16[1,1,32,128]{3,1,2,0:T(2,128)(2,1)S(1)}, u32[]{:S(2)}, u32[]{:S(2)}) collective-permute-start(bf16[1,1,32,128]{3,1,2,0:T(2,128)(2,1)S(1)} %get-tuple-element.154), channel_id=1, source_target_pairs={{1,0},{2,1},{3,2},{5,4},{6,5},{7,6},{9,8},{10,9},{11,10},{13,12},{... | collective-permute-start | bytes 24584 | tf_op jit(solution)/shard_map/while/body/eval_jaxpr/ppermute | solution.py:31
  481.6 7.4 %collective-permute-start = (bf16[1,1,32,128]{3,1,2,0:T(2,128)(2,1)S(1)}, bf16[1,1,32,128]{3,1,2,0:T(2,128)(2,1)S(1)}, u32[]{:S(2)}, u32[]{:S(2)}) collective-permute-start(bf16[1,1,32,128]{3,1,2,0:T(2,128)(2,1)S(1)} %get-tuple-element.154), channel_id=1, source_target_pairs={{1,0},{2,1},{3,2},{5,4},{6,5},{7,6},{9,8},{10,9},{11,10},{13,12},{... | collective-permute-start | bytes 24584 | tf_op jit(solution)/shard_map/while/body/eval_jaxpr/ppermute | solution.py:31
  504.6 7.4 %collective-permute-start = (bf16[1,1,32,128]{3,1,2,0:T(2,128)(2,1)S(1)}, bf16[1,1,32,128]{3,1,2,0:T(2,128)(2,1)S(1)}, u32[]{:S(2)}, u32[]{:S(2)}) collective-permute-start(bf16[1,1,32,128]{3,1,2,0:T(2,128)(2,1)S(1)} %get-tuple-element.154), channel_id=1, source_target_pairs={{1,0},{2,1},{3,2},{5,4},{6,5},{7,6},{9,8},{10,9},{11,10},{13,12},{... | collective-permute-start | bytes 24584 | tf_op jit(solution)/shard_map/while/body/eval_jaxpr/ppermute | solution.py:31
  527.7 7.4 %collective-permute-start = (bf16[1,1,32,128]{3,1,2,0:T(2,128)(2,1)S(1)}, bf16[1,1,32,128]{3,1,2,0:T(2,128)(2,1)S(1)}, u32[]{:S(2)}, u32[]{:S(2)}) collective-permute-start(bf16[1,1,32,128]{3,1,2,0:T(2,128)(2,1)S(1)} %get-tuple-element.154), channel_id=1, source_target_pairs={{1,0},{2,1},{3,2},{5,4},{6,5},{7,6},{9,8},{10,9},{11,10},{13,12},{... | collective-permute-start | bytes 24584 | tf_op jit(solution)/shard_map/while/body/eval_jaxpr/ppermute | solution.py:31
  550.8 7.4 %collective-permute-start = (bf16[1,1,32,128]{3,1,2,0:T(2,128)(2,1)S(1)}, bf16[1,1,32,128]{3,1,2,0:T(2,128)(2,1)S(1)}, u32[]{:S(2)}, u32[]{:S(2)}) collective-permute-start(bf16[1,1,32,128]{3,1,2,0:T(2,128)(2,1)S(1)} %get-tuple-element.154), channel_id=1, source_target_pairs={{1,0},{2,1},{3,2},{5,4},{6,5},{7,6},{9,8},{10,9},{11,10},{13,12},{... | collective-permute-start | bytes 24584 | tf_op jit(solution)/shard_map/while/body/eval_jaxpr/ppermute | solution.py:31
  573.8 7.4 %collective-permute-start = (bf16[1,1,32,128]{3,1,2,0:T(2,128)(2,1)S(1)}, bf16[1,1,32,128]{3,1,2,0:T(2,128)(2,1)S(1)}, u32[]{:S(2)}, u32[]{:S(2)}) collective-permute-start(bf16[1,1,32,128]{3,1,2,0:T(2,128)(2,1)S(1)} %get-tuple-element.154), channel_id=1, source_target_pairs={{1,0},{2,1},{3,2},{5,4},{6,5},{7,6},{9,8},{10,9},{11,10},{13,12},{... | collective-permute-start | bytes 24584 | tf_op jit(solution)/shard_map/while/body/eval_jaxpr/ppermute | solution.py:31
  (167 other events, 915.3 us)
where the time goes:
time: 608 us; the launch traced here: 599 us
  starting transfers between devices  302 us (50%)
  local copies, waits for them, and re-layouts  119 us (20%)
  matrix products  104 us (17%)
  other arithmetic  47.5 us (8%)
  waiting for transfers between devices  21.5 us (4%)
    ppermute x50, starting transfers between devices, edge_exchange(): from_prev = lax.ppermute(high_part, axis_name, forward)  234 us
    conv_general_dilated x48, matrix products, conv_valid(): lax.conv_general_dilated(operand, kernel, (1, 1), 'VALID', dimension_numb...  104 us
    ppermute x50, starting transfers between devices, edge_exchange(): from_next = lax.ppermute(low_part, axis_name, backward)  68.2 us
    dynamic_update_slice x24, local copies, waits for them, and re-layouts, local_run(): lax.scan(time_step, (h_init, c_init), frames_ext)  23 us
    squeeze x48, local copies, waits for them, and re-layouts, local_run(): lax.scan(time_step, (h_init, c_init), frames_ext)  22.9 us
    div x24, other arithmetic, cell_update(): jax.nn.sigmoid(gate_f) * c_prev + jax.nn.sigmoid(gate_i) * jnp.tanh(gate_g)  21.5 us
    ppermute x50, waiting for transfers between devices, edge_exchange(): from_prev = lax.ppermute(high_part, axis_name, forward)  20 us
    conv_general_dilated x96, local copies, waits for them, and re-layouts, conv_valid(): lax.conv_general_dilated(operand, kernel, (1, 1), 'VALID', dimension_numb...  15.6 us
  transfers between devices with their start and end apart: 100, of which 26 were waited for; matrix products, arithmetic and copies ran while one was open for 8% of the time, Pallas kernels for 0%

commit v1 on v0

v1 whole, which is shorter than its diff:
```python
import functools

import jax
import jax.numpy as jnp
from jax import lax
from jax.experimental import pallas as pl
from jax.experimental.pallas import tpu as pltpu
from jax.sharding import PartitionSpec as P

MESH = pl.DeviceIdType.MESH
BF16 = jnp.bfloat16
F32 = jnp.float32

PITCH = 36
DIRECTIONS = ((-1, 0), (1, 0), (0, -1), (0, 1), (-1, -1), (-1, 1), (1, -1), (1, 1))


def opposite(d):
    return DIRECTIONS.index((-DIRECTIONS[d][0], -DIRECTIONS[d][1]))


def cell(r, c):
    return (r + 2) * PITCH + c + 2


def kernel(steps, rows, cols, n_rows, n_cols, frames_ref, w_ref, h0_ref, c0_ref, seq_ref, cout_ref,
           x_buf, p_buf, w_buf, c_main, c_side, out_buf, row_send, col_send, corner_send, row_recv, col_recv,
           corner_recv, send_sem, recv_sem, p_sem, out_sem):
    my_row = lax.axis_index("rows")
    my_col = lax.axis_index("cols")

    def exists(d):
        dr, dc = DIRECTIONS[d]
        ok = None
        for here, step, count in ((my_row, dr, n_rows), (my_col, dc, n_cols)):
            if step:
                this = (here > 0) if step < 0 else (here < count - 1)
                ok = this if ok is None else jnp.logical_and(ok, this)
        return ok

    def device(d):
        dr, dc = DIRECTIONS[d]
        return {"rows": my_row + dr, "cols": my_col + dc}

    row_recv[...] = jnp.zeros_like(row_recv)
    col_recv[...] = jnp.zeros_like(col_recv)
    corner_recv[...] = jnp.zeros_like(corner_recv)

    barrier = pltpu.get_barrier_semaphore()
    count = jnp.int32(0)
    for d in range(8):
        @pl.when(exists(d))
        def _():
            pl.semaphore_signal(barrier, inc=1, device_id=device(d), device_id_type=MESH)
        count = count + exists(d).astype(jnp.int32)
    pl.semaphore_wait(barrier, count)

    def frame_copy(t, slot):
        return pltpu.make_async_copy(frames_ref.at[t], p_buf.at[slot], p_sem.at[slot])

    def out_copy(t, slot):
        return pltpu.make_async_copy(out_buf.at[slot], seq_ref.at[t], out_sem.at[slot])

    def halo_copy(slot, d):
        dr, dc = DIRECTIONS[d]
        if dr and dc:
            src, dst = corner_send.at[slot, d - 4], corner_recv.at[slot, opposite(d) - 4]
        elif dr:
            src, dst = row_send.at[slot, d], row_recv.at[slot, opposite(d)]
        else:
            src, dst = col_send.at[slot, d - 2], col_recv.at[slot, opposite(d) - 2]
        return pltpu.make_async_remote_copy(
            src_ref=src, dst_ref=dst, send_sem=send_sem.at[slot, d], recv_sem=recv_sem.at[slot, opposite(d)],
            device_id=device(d), device_id_type=MESH)

    def arrival(slot, d):
        if d >= 4:
            src, dst = corner_send.at[slot, d - 4], corner_recv.at[slot, d - 4]
        elif d < 2:
            src, dst = row_send.at[slot, d], row_recv.at[slot, d]
        else:
            src, dst = col_send.at[slot, d - 2], col_recv.at[slot, d - 2]
        return pltpu.make_async_remote_copy(
            src_ref=src, dst_ref=dst, send_sem=send_sem.at[slot, d], recv_sem=recv_sem.at[slot, d],
            device_id=device(d), device_id_type=MESH)

    frame_copy(0, 0).start()
    frame_copy(1, 1).start()
    x_buf[...] = jnp.zeros_like(x_buf)
    w_buf[...] = w_ref[...]

    side_cols = (0, 1, 2, 3, cols - 4, cols - 3, cols - 2, cols - 1)
    width = cols - 8

    for r in range(rows):
        x_buf[0, pl.ds(cell(r, 0), cols), :] = h0_ref[r].astype(F32)
        c_main[pl.ds(r * width, width), :] = c0_ref[r, 4:cols - 4, :]
    c_flat = c0_ref.reshape(rows * cols, 128)
    for i, c in enumerate(side_cols):
        c_side[pl.ds(i * rows, rows), :] = c_flat[pl.ds(c, rows, stride=cols), :]

    def lhs_of(slot, groups):
        parts = []
        for dy in range(3):
            for dx in range(3):
                pieces = []
                for r, c, length, vertical in groups:
                    start = cell(r + dy - 1, c + dx - 1)
                    index = pl.ds(start, length, stride=PITCH) if vertical else pl.ds(start, length)
                    pieces.append(x_buf[slot, index, :])
                parts.append(jnp.concatenate(pieces, axis=0) if len(pieces) > 1 else pieces[0])
        for dy in range(3):
            pieces = []
            for r, c, length, vertical in groups:
                start = (r + dy) * cols + c
                index = pl.ds(start, length, stride=cols) if vertical else pl.ds(start, length)
                pieces.append(p_buf[slot, index, :])
            parts.append(jnp.concatenate(pieces, axis=0) if len(pieces) > 1 else pieces[0])
        return jnp.concatenate(parts, axis=1).astype(BF16)

    def gates_of(slot, groups):
        return jnp.dot(lhs_of(slot, groups), w_buf[...], preferred_element_type=F32)

    def update(gates, c_prev):
        gi, gf, go, gg = (jnp.tanh(gates[:, 128 * k:128 * (k + 1)]) for k in range(4))
        c_next = 0.5 * ((gf * c_prev + c_prev) + (gi * gg + gg))
        return (0.5 * go + 0.5) * jnp.tanh(c_next), c_next

    def send_halo(slot, wanted=True):
        nxt = x_buf.at[slot]
        for k, r in enumerate((0, rows - 1)):
            row_send[slot, k] = nxt[pl.ds(cell(r, 0), cols), :].astype(BF16)
        for k, c in enumerate((0, cols - 1)):
            col_send[slot, k] = nxt[pl.ds(cell(0, c), rows, stride=PITCH), :].astype(BF16)
        for k, (dr, dc) in enumerate(DIRECTIONS[4:]):
            r = 0 if dr < 0 else rows - 1
            c = 0 if dc < 0 else cols - 1
            corner_send[slot, k] = jnp.broadcast_to(nxt[pl.ds(cell(r, c), 1), :], (16, 128)).astype(BF16)
        for d in range(8):
            @pl.when(jnp.logical_and(exists(d), wanted))
            def _():
                halo_copy(slot, d).start()

    def wait_halo(slot):
        for d in range(8):
            @pl.when(exists(d))
            def _():
                arrival(slot, d).wait_recv()
        now = x_buf.at[slot]
        for k, r in enumerate((-1, rows)):
            now[pl.ds(cell(r, 0), cols), :] = row_recv[slot, k].astype(F32)
        for k, c in enumerate((-1, cols)):
            now[pl.ds(cell(0, c), rows, stride=PITCH), :] = col_recv[slot, k].astype(F32)
        for k, (dr, dc) in enumerate(DIRECTIONS[4:]):
            r = -1 if dr < 0 else rows
            c = -1 if dc < 0 else cols
            now[pl.ds(cell(r, c), 1), :] = corner_recv[slot, k][0:1, :].astype(F32)

    def wait_sent(slot):
        for d in range(8):
            @pl.when(exists(d))
            def _():
                halo_copy(slot, d).wait_send()

    def side_run(i):
        return (0, side_cols[i], rows, True)

    def do_side(now, ids):
        gates = gates_of(now, [side_run(i) for i in ids])
        if len(ids) == ids[-1] - ids[0] + 1:
            c_index = pl.ds(ids[0] * rows, len(ids) * rows)
            h, c_next = update(gates, c_side[c_index, :])
            c_side[c_index, :] = c_next
        else:
            c_prev = jnp.concatenate([c_side[pl.ds(i * rows, rows), :] for i in ids], axis=0)
            h, c_next = update(gates, c_prev)
            for n, i in enumerate(ids):
                c_side[pl.ds(i * rows, rows), :] = c_next[n * rows:(n + 1) * rows]
        for n, i in enumerate(ids):
            x_buf[1 - now, pl.ds(cell(0, side_cols[i]), rows, stride=PITCH), :] = h[n * rows:(n + 1) * rows]

    def do_main(now, row_list):
        gates = gates_of(now, [(r, 4, width, False) for r in row_list])
        if len(row_list) == row_list[-1] - row_list[0] + 1:
            c_index = pl.ds(row_list[0] * width, len(row_list) * width)
            h, c_next = update(gates, c_main[c_index, :])
            c_main[c_index, :] = c_next
        else:
            c_prev = jnp.concatenate([c_main[pl.ds(r * width, width), :] for r in row_list], axis=0)
            h, c_next = update(gates, c_prev)
            for n, r in enumerate(row_list):
                c_main[pl.ds(r * width, width), :] = c_next[n * width:(n + 1) * width]
        for n, r in enumerate(row_list):
            x_buf[1 - now, pl.ds(cell(r, 4), width), :] = h[n * width:(n + 1) * width]

    def one_step(t, now):
        frame_copy(t, now).wait()
        wait_halo(now)

        @pl.when(t >= 1)
        def _():
            wait_sent(1 - now)

        do_side(now, (0, 1, 2, 3))
        do_side(now, (4, 5, 6, 7))
        do_main(now, (0, rows - 1))
        send_halo(1 - now, t + 1 < steps)
        inner = list(range(1, rows - 1))
        block = 12
        for at in range(0, len(inner), block):
            do_main(now, inner[at:at + block])

        @pl.when(t + 2 < steps)
        def _():
            frame_copy(t + 2, now).start()

        @pl.when(t >= 2)
        def _():
            out_copy(t - 2, now).wait()
        for r in range(rows):
            out_buf[now, r] = x_buf[1 - now, pl.ds(cell(r, 0), cols), :].astype(BF16)
        out_copy(t, now).start()

    send_halo(0)

    def two_steps(i, carry):
        one_step(2 * i, 0)
        one_step(2 * i + 1, 1)
        return carry

    lax.fori_loop(0, steps // 2, two_steps, 0)

    wait_sent(1)
    out_copy(steps - 2, 0).wait()
    out_copy(steps - 1, 1).wait()
    for r in range(rows):
        cout_ref[r, 4:cols - 4, :] = c_main[pl.ds(r * width, width), :]
    cout_flat = cout_ref.reshape(rows * cols, 128)
    for i, c in enumerate(side_cols):
        cout_flat[pl.ds(c, rows, stride=cols), :] = c_side[pl.ds(i * rows, rows), :]


def edge_exchange(tile_in, axis_name, axis_size, axis_dim, width):
    length = tile_in.shape[axis_dim]
    low_part = lax.slice_in_dim(tile_in, 0, width, axis=axis_dim)
    high_part = lax.slice_in_dim(tile_in, length - width, length, axis=axis_dim)
    forward = [(source, source + 1) for source in range(axis_size - 1)]
    backward = [(source + 1, source) for source in range(axis_size - 1)]
    from_prev = lax.ppermute(high_part, axis_name, forward)
    from_next = lax.ppermute(low_part, axis_name, backward)
    return jnp.concatenate([from_prev, tile_in, from_next], axis=axis_dim)


def solution(mesh):
    n_rows = mesh.shape["rows"]
    n_cols = mesh.shape["cols"]
    seq_spec = P(None, "dp", "rows", "cols", None)
    state_spec = P("dp", "rows", "cols", None)

    def local_run(frames, w_in, w_rec, gate_bias, h_init, c_init):
        steps, _, rows, cols, c_in = frames.shape
        hid = h_init.shape[-1]
        ext = edge_exchange(edge_exchange(frames, "rows", n_rows, 2, 1), "cols", n_cols, 3, 1)[:, 0]
        ones = jnp.zeros((steps, rows + 2, cols, 128 - 3 * c_in), BF16).at[..., :3].set(1)
        packed = jnp.concatenate([ext[:, :, dx:dx + cols] for dx in range(3)] + [ones], axis=-1)
        packed = packed.astype(F32).reshape(steps, (rows + 2) * cols, 128)

        scale = jnp.concatenate([jnp.full((3 * hid,), 0.5, F32), jnp.ones((hid,), F32)])
        bias = gate_bias * scale
        b0 = lax.reduce_precision(bias, 8, 7)
        b1 = lax.reduce_precision(bias - b0, 8, 7)
        b2 = lax.reduce_precision(bias - b0 - b1, 8, 7)
        w_pad = jnp.zeros((128 - 3 * c_in, 4 * hid), F32)
        blocks = [w_rec.astype(F32).reshape(9 * hid, 4 * hid) * scale]
        for dy in range(3):
            rest = w_pad if dy else jnp.concatenate([jnp.stack([b0, b1, b2]), w_pad[3:]], axis=0)
            blocks += [w_in[dy].astype(F32).reshape(3 * c_in, 4 * hid) * scale, rest]
        w_all = jnp.concatenate(blocks, axis=0).astype(BF16)

        vmem = pl.BlockSpec(memory_space=pltpu.VMEM)
        anywhere = pl.BlockSpec(memory_space=pl.ANY)
        seq, c_last = pl.pallas_call(
            functools.partial(kernel, steps, rows, cols, n_rows, n_cols),
            out_shape=(jax.ShapeDtypeStruct((steps, rows, cols, hid), BF16),
                       jax.ShapeDtypeStruct((rows, cols, hid), F32)),
            in_specs=[anywhere, vmem, vmem, vmem],
            out_specs=(anywhere, vmem),
            scratch_shapes=[
                pltpu.VMEM((2, (rows + 4) * PITCH, 128), F32),
                pltpu.VMEM((2, (rows + 2) * cols, 128), F32),
                pltpu.VMEM((1536, 4 * hid), BF16),
                pltpu.VMEM((rows * (cols - 8), 128), F32),
                pltpu.VMEM((rows * 8, 128), F32),
                pltpu.VMEM((2, rows, cols, 128), BF16),
                pltpu.VMEM((2, 2, cols, 128), BF16),
                pltpu.VMEM((2, 2, rows, 128), BF16),
                pltpu.VMEM((2, 4, 16, 128), BF16),
                pltpu.VMEM((2, 2, cols, 128), BF16),
                pltpu.VMEM((2, 2, rows, 128), BF16),
                pltpu.VMEM((2, 4, 16, 128), BF16),
                pltpu.SemaphoreType.DMA((2, 8)),
                pltpu.SemaphoreType.DMA((2, 8)),
                pltpu.SemaphoreType.DMA((2,)),
                pltpu.SemaphoreType.DMA((2,)),
            ],
            compiler_params=pltpu.CompilerParams(
                collective_id=0, has_side_effects=True, vmem_limit_bytes=48 * 2**20),
            name="convlstm",
        )(packed, w_all, h_init[0], c_init[0])
        return seq[:, None], c_last[None]

    return jax.shard_map(local_run, mesh=mesh, in_specs=(seq_spec, P(), P(), P(), state_spec, state_spec),
                         out_specs=(seq_spec, state_spec), check_vma=False)
```

time: 608 us -> 233 us (0.38); the launches traced: 599 us -> 231 us
  starting transfers between devices: 302 us -> 9.49 us
  Pallas kernels: 0 us -> 109 us
  matrix products: 104 us -> 0 us
  local copies, waits for them, and re-layouts: 119 us -> 77.7 us
  waiting for transfers between devices: 21.5 us -> 0.02 us
  other arithmetic: 47.5 us -> 34 us
    ppermute x50 -> x2, starting transfers between devices: 234 us -> 6.74 us  [edge_exchange(): from_prev = lax.ppermute(high_part, axis_name, forward)]
    pallas_call x0 -> x1, Pallas kernels: none -> 109 us  [local_run(): pl.pallas_call(functools.partial(kernel, steps, rows, cols, n_rows, n_col...]
    conv_general_dilated x48 -> x0, matrix products: 104 us -> none  [conv_valid(): lax.conv_general_dilated(operand, kernel, (1, 1), 'VALID', dimension_numb...]
    ppermute x50 -> x2, starting transfers between devices: 68.2 us -> 2.75 us  [edge_exchange(): from_next = lax.ppermute(low_part, axis_name, backward)]
    slice x0 -> x6, local copies, waits for them, and re-layouts: none -> 39.7 us  [the longest x4 39.7 us: local_run(): ext[:, :, dx:dx + cols]]
    dynamic_update_slice x24 -> x0, local copies, waits for them, and re-layouts: 23 us -> none  [local_run(): lax.scan(time_step, (h_init, c_init), frames_ext)]
    squeeze x48 -> x0, local copies, waits for them, and re-layouts: 22.9 us -> none  [local_run(): lax.scan(time_step, (h_init, c_init), frames_ext)]
    div x24 -> x0, other arithmetic: 21.5 us -> none  [cell_update(): jax.nn.sigmoid(gate_f) * c_prev + jax.nn.sigmoid(gate_i) * jnp.tanh(gate_g)]
  transfers between devices with their start and end apart: 100 -> 4, of which waited for: 26 -> 0; matrix products, arithmetic and copies ran while one was open for 8% -> 6% of each run, Pallas kernels for 0% -> 0%
where the time goes in v1:
time: 233 us; the launch traced here: 231 us
  Pallas kernels  109 us (47%)
  local copies, waits for them, and re-layouts  77.7 us (33%)
  other arithmetic  34 us (15%)
  starting transfers between devices  9.49 us (4%)
    pallas_call x1, Pallas kernels, local_run(): pl.pallas_call(functools.partial(kernel, steps, rows, cols, n_rows, n_col...  109 us
    slice x4, local copies, waits for them, and re-layouts, local_run(): ext[:, :, dx:dx + cols]  39.7 us
    convert_element_type x1, other arithmetic, local_run(): packed = packed.astype(F32).reshape(steps, (rows + 2) * cols, 128)  24.8 us
    unnamed x16, local copies, waits for them, and re-layouts  18.6 us
    ppermute x2, starting transfers between devices, edge_exchange(): from_prev = lax.ppermute(high_part, axis_name, forward)  6.74 us
    slice x1, local copies, waits for them, and re-layouts, edge_exchange(): high_part = lax.slice_in_dim(tile_in, length - width, length, axis=axis_dim)  6 us
    squeeze x1, other arithmetic, local_run(): edge_exchange(edge_exchange(frames, 'rows', n_rows, 2, 1), 'cols', n_cols...  5.31 us
    concatenate x1, local copies, waits for them, and re-layouts, local_run(): w_all = jnp.concatenate(blocks, axis=0).astype(BF16)  4.91 us
  transfers between devices with their start and end apart: 4, of which 0 were waited for; matrix products, arithmetic and copies ran while one was open for 6% of the time, Pallas kernels for 0%

profile of v1, /device:TPU:0, one launch (start us, length us, event | category | flops | bytes accessed | tf_op | source)
XLA Modules:
  0.0 231.1 jit_solution(6802574432527927647)
XLA Ops:
  0.6 6.0 %fusion.7 = (bf16[24,1,1,32,16]{2,4,3,1,0:T(8,128)(2,1)}, bf16[24,1,1,32,16]{2,4,3,1,0:T(8,128)(2,1)S(1)}) fusion(bf16[24,1,48,32,16]{2,4,3,1,0:T(8,128)(2,1)} %param.8), kind=kLoop, calls=%fused_computation.20 | loop fusion | bytes 98304 | tf_op jit(solution)/shard_map/slice | solution.py:246
  6.6 0.0 copy-start.3
  6.6 4.3 %copy.20 = bf16[24,1,1,32,16]{3,4,2,1,0:T(8,128)(2,1)S(1)} copy(bf16[24,1,1,32,16]{2,4,3,1,0:T(8,128)(2,1)} %get-tuple-element.27) | data formatting | bytes 49152
  11.0 2.4 %collective-permute-start = (bf16[24,1,1,32,16]{3,4,2,1,0:T(8,128)(2,1)S(1)}, bf16[24,1,1,32,16]{3,4,2,1,0:T(8,128)(2,1)S(1)}, u32[]{:S(2)}, u32[]{:S(2)}) collective-permute-start(bf16[24,1,1,32,16]{3,4,2,1,0:T(8,128)(2,1)S(1)} %copy.20), channel_id=1, source_target_pairs={{0,1},{1,2},{2,3},{4,5},{5,6},{6,7},{8,9},{9,10},{10,11},{12,13},{... | collective-permute-start | bytes 73736 | tf_op jit(solution)/shard_map/ppermute | solution.py:249
  13.4 3.5 %copy.21 = bf16[24,1,1,32,16]{3,4,2,1,0:T(8,128)(2,1)} copy(bf16[24,1,1,32,16]{2,4,3,1,0:T(8,128)(2,1)S(1)} %get-tuple-element.28) | data formatting | bytes 49152
  16.9 1.3 collective-permute-start.1
  18.2 0.0 copy-done.3
  18.2 0.0 copy-done.4
  18.3 2.5 %fusion = bf16[1152,512]{1,0:T(8,128)(2,1)} fusion(bf16[3,3,128,512]{3,2,1,0:T(8,128)(2,1)} %param.10, f32[512]{0:T(512)S(1)} %copy-done.4), kind=kLoop, calls=%fused_computation.3 | loop fusion | flops 1769472 | bytes 2361344 | tf_op jit(solution)/shard_map/convert.4
  20.8 0.0 collective-permute-done
  20.8 3.9 %copy.14 = bf16[24,1,1,32,16]{2,4,3,1,0:T(8,128)(2,1)} copy(bf16[24,1,1,32,16]{3,4,2,1,0:T(8,128)(2,1)S(1)} %collective-permute-done) | data formatting | bytes 49152 | tf_op jit(solution)/shard_map/ppermute | solution.py:249
  24.7 0.0 collective-permute-done.1
  24.7 4.6 %copy.15 = bf16[24,1,1,32,16]{2,4,3,1,0:T(8,128)(2,1)} copy(bf16[24,1,1,32,16]{3,4,2,1,0:T(8,128)(2,1)} %collective-permute-done.1) | data formatting | bytes 49152 | tf_op jit(solution)/shard_map/ppermute | solution.py:250
  29.3 0.0 copy-done.2
  29.3 1.2 pad_maximum_fusion.2
  30.5 4.3 %collective-permute-start.2 = (bf16[24,1,50,1,16]{2,4,3,1,0:T(8,128)(2,1)S(1)}, bf16[24,1,50,1,16]{2,4,3,1,0:T(8,128)(2,1)S(1)}, u32[]{:S(2)}, u32[]{:S(2)}) collective-permute-start(bf16[24,1,50,1,16]{2,4,3,1,0:T(8,128)(2,1)S(1)} %get-tuple-element.22), channel_id=1, source_target_pairs={{0,4},{4,8},{8,12},{1,5},{5,9},{9,13},{2,6},{6,10},{10,14},{3,7},{... | collective-permute-start | bytes 115208 | tf_op jit(solution)/shard_map/ppermute | solution.py:249
  34.9 1.5 collective-permute-start.3
  36.3 0.0 copy-done.5
  36.4 4.9 %concatenate.28.w_ref = bf16[1536,512]{1,0:T(8,128)(2,1)S(1)} concatenate(bf16[1152,512]{1,0:T(8,128)(2,1)} %fusion, bf16[48,512]{1,0:T(8,128)(2,1)S(1)} %get-tuple-element.37, bf16[1,512]{1,0:T(2,128)(2,1)S(1)} %stack.12, bf16[1,512]{1,0:T(2,128)(2,1)S(1)} %stack.13, bf16[1,512]{1,0:T(2,128)(2,1)S(1)} %stack.14, bf16[77,512]{1,0:T(8,128)(2,1)S(1)} %slice.67, ...), dimensions={0} | concatenate | bytes 3145728 | tf_op jit(solution)/shard_map/concatenate | solution.py:278
  41.3 0.0 collective-permute-done.2
  41.4 0.0 collective-permute-done.3
  41.4 5.3 %maximum_bitcast_fusion = bf16[24,50,34,16]{1,3,2,0:T(8,128)(2,1)S(1)} fusion(bf16[24,1,50,1,16]{2,4,3,1,0:T(8,128)(2,1)S(1)} %collective-permute-done.3, bf16[24,1,1,32,16]{2,4,3,1,0:T(8,128)(2,1)} %copy.15, bf16[24,1,48,32,16]{2,4,3,1,0:T(8,128)(2,1)} %param.8, bf16[24,1,1,32,16]{2,4,3,1,0:T(8,128)(2,1)} %copy.14, ...), kind=kLoop, calls=%fused_computation.1 | loop fusion | flops 6528000 | bytes 2611200 | tf_op jit(solution)/shard_map/squeeze | solution.py:263
  46.7 4.4 %fusion.6 = (bf16[24,50,32,16]{1,3,2,0:T(8,128)(2,1)}, bf16[24,50,32,16]{1,3,2,0:T(8,128)(2,1)}, bf16[24,50,32,16]{1,3,2,0:T(8,128)(2,1)}) fusion(bf16[24,50,34,16]{1,3,2,0:T(8,128)(2,1)S(1)} %maximum_bitcast_fusion), kind=kLoop, calls=%fused_computation.19 | loop fusion | bytes 7372800 | tf_op jit(solution)/shard_map/slice | solution.py:265
  51.1 11.8 %copy.16 = bf16[24,50,32,16]{3,2,1,0:T(8,128)(2,1)} copy(bf16[24,50,32,16]{1,3,2,0:T(8,128)(2,1)} %get-tuple-element.24) | data formatting | bytes 2457600 | tf_op jit(solution)/shard_map/slice | solution.py:265
  62.9 11.8 %copy.17 = bf16[24,50,32,16]{3,2,1,0:T(8,128)(2,1)} copy(bf16[24,50,32,16]{1,3,2,0:T(8,128)(2,1)} %get-tuple-element.26) | data formatting | bytes 2457600 | tf_op jit(solution)/shard_map/slice | solution.py:265
  74.6 11.7 %copy.18 = bf16[24,50,32,16]{3,2,1,0:T(8,128)(2,1)} copy(bf16[24,50,32,16]{1,3,2,0:T(8,128)(2,1)} %get-tuple-element.25) | data formatting | bytes 2457600 | tf_op jit(solution)/shard_map/slice | solution.py:265
  86.4 24.8 %maximum_convert_fusion.frames_ref = f32[24,1600,128]{2,1,0:T(8,128)} fusion(bf16[24,1600,80]{2,1,0:T(8,128)(2,1)} %constant.36.clone.1, bf16[24,1600,16]{2,1,0:T(8,128)(2,1)} %bitcast.28, bf16[24,1600,16]{2,1,0:T(8,128)(2,1)} %bitcast.27, bf16[24,1600,16]{2,1,0:T(8,128)(2,1)} %bitcast.26), kind=kLoop, calls=%fused_computation | loop fusion | flops 39321600 | bytes 29491200 | tf_op jit(solution)/shard_map/convert_element_type | solution.py:266
  111.2 0.0 copy-done
  111.2 0.0 copy-done.1
  111.2 109.2 %convlstm.1 = (bf16[24,48,32,128]{3,2,1,0:T(8,128)(2,1)}, f32[48,32,128]{2,1,0:T(8,128)S(1)}) custom-call(f32[24,1600,128]{2,1,0:T(8,128)} %maximum_convert_fusion.frames_ref, bf16[1536,512]{1,0:T(8,128)(2,1)S(1)} %concatenate.28.w_ref, bf16[48,32,128]{2,1,0:T(8,128)(2,1)S(1)} %bitcast.25, f32[48,32,128]{2,1,0:T(8,128)S(1)} %bitcast.23), custom_call_target="tpu_custom_call" | custom-call | tf_op jit(solution)/shard_map/convlstm/pallas_call | solution.py:282
  220.4 9.9 %copy.24 = bf16[24,1,48,32,128]{4,3,2,1,0:T(8,128)(2,1)} copy(bf16[24,1,48,32,128]{4,3,2,1,0:T(8,128)(2,1)} %bitcast.29) | data formatting | bytes 18874368
  230.3 0.9 copy.25
  (13 shorter events, 0.1 us)
Async XLA Ops:
  6.6 11.6 %copy-start.3 = (bf16[3,3,16,512]{3,2,1,0:T(8,128)(2,1)S(1)}, bf16[3,3,16,512]{3,2,1,0:T(8,128)(2,1)}, u32[]{:S(2)}) copy-start(bf16[3,3,16,512]{3,2,1,0:T(8,128)(2,1)} %param.9) | copy-start | bytes 442372
  6.6 11.6 %copy-start.4 = (f32[512]{0:T(512)S(1)}, f32[512]{0:T(512)}, u32[]{:S(2)}) copy-start(f32[512]{0:T(512)} %constant.37.clone.1) | copy-start | bytes 6148
  11.0 9.9 %collective-permute-start = (bf16[24,1,1,32,16]{3,4,2,1,0:T(8,128)(2,1)S(1)}, bf16[24,1,1,32,16]{3,4,2,1,0:T(8,128)(2,1)S(1)}, u32[]{:S(2)}, u32[]{:S(2)}) collective-permute-start(bf16[24,1,1,32,16]{3,4,2,1,0:T(8,128)(2,1)S(1)} %copy.20), channel_id=1, source_target_pairs={{0,1},{1,2},{2,3},{4,5},{5,6},{6,7},{8,9},{9,10},{10,11},{12,13},{... | collective-permute-start | bytes 73736 | tf_op jit(solution)/shard_map/ppermute | solution.py:249
  16.9 7.8 %collective-permute-start.1 = (bf16[24,1,1,32,16]{3,4,2,1,0:T(8,128)(2,1)}, bf16[24,1,1,32,16]{3,4,2,1,0:T(8,128)(2,1)}, u32[]{:S(2)}, u32[]{:S(2)}) collective-permute-start(bf16[24,1,1,32,16]{3,4,2,1,0:T(8,128)(2,1)} %copy.21), channel_id=1, source_target_pairs={{1,0},{2,1},{3,2},{5,4},{6,5},{7,6},{9,8},{10,9},{11,10},{13,12},{... | collective-permute-start | bytes 73736 | tf_op jit(solution)/shard_map/ppermute | solution.py:250
  20.8 8.5 %copy-start.2 = (bf16[24,1,48,32,16]{2,4,3,1,0:T(8,128)(2,1)S(1)}, bf16[24,1,48,32,16]{2,4,3,1,0:T(8,128)(2,1)}, u32[]{:S(2)}) copy-start(bf16[24,1,48,32,16]{2,4,3,1,0:T(8,128)(2,1)} %param.8) | copy-start | bytes 3538948
  29.3 7.1 %copy-start.5 = (f32[512]{0:T(512)S(1)}, f32[512]{0:T(512)}, u32[]{:S(2)}) copy-start(f32[512]{0:T(512)} %param.11) | copy-start | bytes 6148
  30.5 10.8 %collective-permute-start.2 = (bf16[24,1,50,1,16]{2,4,3,1,0:T(8,128)(2,1)S(1)}, bf16[24,1,50,1,16]{2,4,3,1,0:T(8,128)(2,1)S(1)}, u32[]{:S(2)}, u32[]{:S(2)}) collective-permute-start(bf16[24,1,50,1,16]{2,4,3,1,0:T(8,128)(2,1)S(1)} %get-tuple-element.22), channel_id=1, source_target_pairs={{0,4},{4,8},{8,12},{1,5},{5,9},{9,13},{2,6},{6,10},{10,14},{3,7},{... | collective-permute-start | bytes 115208 | tf_op jit(solution)/shard_map/ppermute | solution.py:249
  34.9 6.5 %collective-permute-start.3 = (bf16[24,1,50,1,16]{2,4,3,1,0:T(8,128)(2,1)S(1)}, bf16[24,1,50,1,16]{2,4,3,1,0:T(8,128)(2,1)S(1)}, u32[]{:S(2)}, u32[]{:S(2)}) collective-permute-start(bf16[24,1,50,1,16]{2,4,3,1,0:T(8,128)(2,1)S(1)} %get-tuple-element.23), channel_id=1, source_target_pairs={{4,0},{8,4},{12,8},{5,1},{9,5},{13,9},{6,2},{10,6},{14,10},{7,3},{... | collective-permute-start | bytes 115208 | tf_op jit(solution)/shard_map/ppermute | solution.py:250
  86.4 24.8 %copy-start = (f32[1,48,32,128]{3,2,1,0:T(8,128)S(1)}, f32[1,48,32,128]{3,2,1,0:T(8,128)}, u32[]{:S(2)}) copy-start(f32[1,48,32,128]{3,2,1,0:T(8,128)} %param.13) | copy-start | bytes 2359300
  86.4 24.8 %copy-start.1 = (bf16[1,48,32,128]{3,2,1,0:T(8,128)(2,1)S(1)}, bf16[1,48,32,128]{3,2,1,0:T(8,128)(2,1)}, u32[]{:S(2)}) copy-start(bf16[1,48,32,128]{3,2,1,0:T(8,128)(2,1)} %param.12) | copy-start | bytes 1179652

commit v2 on v0

v2 whole, which is shorter than its diff:
```python
import functools

import jax
import jax.numpy as jnp
from jax import lax
from jax.experimental import pallas as pl
from jax.experimental.pallas import tpu as pltpu
from jax.sharding import PartitionSpec as P

MESH = pl.DeviceIdType.MESH
BF16 = jnp.bfloat16
F32 = jnp.float32
TDT = jnp.bfloat16

PITCH = 36
DIRECTIONS = ((-1, 0), (1, 0), (0, -1), (0, 1), (-1, -1), (-1, 1), (1, -1), (1, 1))
SIDE = 4


def cell(r, c):
    return (r + 1) * PITCH + c + 2


def pcell(r, c):
    return (r + 1) * PITCH + c


def kernel(steps, rows, cols, n_rows, n_cols, c_in, frames_ref, w_rec_ref, w_in_ref, bias_ref, h0_ref, c0_ref,
           seq_ref, cout_ref,
           x_buf, p_buf, w_buf, f_buf, f_side, c_main, c_side, c_col, c_row, out_buf, row_send, col_send,
           row_recv, col_recv, corner_recv, send_sem, recv_sem, f_sem, f_send_sem, f_recv_sem, out_sem):
    my_row = lax.axis_index("rows")
    my_col = lax.axis_index("cols")
    hid = x_buf.shape[-1]
    gates_n = 4 * hid
    packed = 3 * c_in
    width = cols - 2 * SIDE
    edge_cols = (0, cols - 1)
    edge_rows = (0, rows - 1)
    inner_side = tuple(range(1, SIDE)) + tuple(range(cols - SIDE, cols - 1))

    def exists(d):
        dr, dc = DIRECTIONS[d]
        ok = None
        for here, step, count in ((my_row, dr, n_rows), (my_col, dc, n_cols)):
            if step:
                this = (here > 0) if step < 0 else (here < count - 1)
                ok = this if ok is None else jnp.logical_and(ok, this)
        return ok

    def device(d):
        dr, dc = DIRECTIONS[d]
        return {"rows": my_row + dr, "cols": my_col + dc}

    def opposite(d):
        return DIRECTIONS.index((-DIRECTIONS[d][0], -DIRECTIONS[d][1]))

    def out_copy(t, slot):
        return pltpu.make_async_copy(out_buf.at[slot], seq_ref.at[t], out_sem.at[slot])

    def source(slot, d):
        dr, dc = DIRECTIONS[d]
        if dr and dc:
            return col_send.at[slot, 0 if dc < 0 else 1, pl.ds(0 if dr < 0 else rows - 16, 16)]
        return row_send.at[slot, d] if dr else col_send.at[slot, d - 2]

    def landing(slot, d):
        dr, dc = DIRECTIONS[d]
        if dr and dc:
            return corner_recv.at[slot, d - 4]
        return row_recv.at[slot, d] if dr else col_recv.at[slot, d - 2]

    def departure(slot, d):
        return pltpu.make_async_remote_copy(
            src_ref=source(slot, d), dst_ref=landing(slot, opposite(d)), send_sem=send_sem.at[slot, d],
            recv_sem=recv_sem.at[slot, opposite(d)], device_id=device(d), device_id_type=MESH)

    def arrival(slot, d):
        return pltpu.make_async_remote_copy(
            src_ref=source(slot, d), dst_ref=landing(slot, d), send_sem=send_sem.at[slot, d],
            recv_sem=recv_sem.at[slot, d], device_id=device(d), device_id_type=MESH)

    def frame_side(part, d, arriving=False):
        ts = pl.ds(0, 1) if part == 0 else pl.ds(1, steps - 1)
        k = d - 2
        at = k if arriving else 1 - k
        return pltpu.make_async_remote_copy(
            src_ref=frames_ref.at[ts, edge_cols[k]], dst_ref=f_side.at[at, ts], send_sem=f_send_sem.at[part, k],
            recv_sem=f_recv_sem.at[part, at], device_id=device(d), device_id_type=MESH)

    def frame_load(part):
        ts = pl.ds(0, 1) if part == 0 else pl.ds(1, steps - 1)
        return pltpu.make_async_copy(frames_ref.at[ts], f_buf.at[ts], f_sem.at[part])

    frame_load(0).start()
    frame_load(1).start()
    row_recv[...] = jnp.zeros_like(row_recv)
    col_recv[...] = jnp.zeros_like(col_recv)
    corner_recv[...] = jnp.zeros_like(corner_recv)
    f_side[...] = jnp.zeros_like(f_side)

    barrier = pltpu.get_barrier_semaphore()
    count = jnp.int32(0)
    for d in range(8):
        @pl.when(exists(d))
        def _():
            pl.semaphore_signal(barrier, inc=1, device_id=device(d), device_id_type=MESH)
        count = count + exists(d).astype(jnp.int32)
    pl.semaphore_wait(barrier, count)

    for part in (0, 1):
        for d in (2, 3):
            @pl.when(exists(d))
            def _():
                frame_side(part, d).start()

    for r in range(rows):
        x_buf[0, pl.ds(cell(r, 0), cols), :] = h0_ref[r].astype(F32)
    for r in range(1, rows - 1):
        c_main[pl.ds((r - 1) * width, width), :] = c0_ref[pl.ds(r * cols + SIDE, width), :]
    for i, c in enumerate(inner_side):
        c_side[pl.ds(i * rows, rows), :] = c0_ref[pl.ds(c, rows, stride=cols), :]
    for i, c in enumerate(edge_cols):
        c_col[pl.ds(i * rows, rows), :] = c0_ref[pl.ds(c, rows, stride=cols), :]
    for i, r in enumerate(edge_rows):
        c_row[pl.ds(i * cols, cols), :] = c0_ref[pl.ds(r * cols, cols), :]

    lane = lax.broadcasted_iota(jnp.int32, (1, gates_n), 1)
    scale = jnp.where(lane < 3 * hid, 0.5, 1.0)
    for at in range(0, 9 * hid, 128):
        w_buf[pl.ds(at, 128), :] = (w_rec_ref[pl.ds(at, 128), :].astype(F32) * scale).astype(BF16)
    bias = bias_ref[...] * scale
    b0 = bias.astype(BF16).astype(F32)
    b1 = (bias - b0).astype(BF16).astype(F32)
    b2 = bias - b0 - b1
    row = lax.broadcasted_iota(jnp.int32, (16, gates_n), 0)
    bias_rows = jnp.where(row == 0, b0, jnp.where(row == 1, b1, jnp.where(row == 2, b2, 0.0)))
    for dy in range(3):
        at = 9 * hid + 128 * dy
        w_buf[pl.ds(at, packed), :] = (w_in_ref[pl.ds(packed * dy, packed), :].astype(F32) * scale).astype(BF16)
        w_buf[pl.ds(at + packed, 128 - packed), :] = jnp.zeros((128 - packed, gates_n), BF16)
        if dy == 1:
            w_buf[pl.ds(at + packed, 16), :] = bias_rows.astype(BF16)

    row = lax.broadcasted_iota(jnp.int32, (128 - packed, rows), 0)
    ones = jnp.where(row < 3, 1.0, 0.0).astype(TDT)

    def pack_frame(t, slot):
        for c in range(cols):
            if c == 0:
                window = jnp.concatenate([f_side[0, t], f_buf[t, 0], f_buf[t, 1]], axis=0)
            elif c == cols - 1:
                window = jnp.concatenate([f_buf[t, c - 1], f_buf[t, c], f_side[1, t]], axis=0)
            else:
                window = f_buf[t, c - 1:c + 2].reshape(packed, rows)
            window = jnp.concatenate([window.astype(TDT), ones], axis=0)
            p_buf[slot, pl.ds(pcell(0, c), rows, stride=PITCH), :] = window.T.astype(F32)

    def lhs_of(slot, groups):
        parts = []
        for dy in range(3):
            for dx in range(3):
                pieces = []
                for r, c, length, vertical in groups:
                    start = cell(r + dy - 1, c + dx - 1)
                    index = pl.ds(start, length, stride=PITCH) if vertical else pl.ds(start, length)
                    pieces.append(x_buf[slot, index, :])
                parts.append(jnp.concatenate(pieces, axis=0) if len(pieces) > 1 else pieces[0])
        for dy in range(3):
            pieces = []
            for r, c, length, vertical in groups:
                start = pcell(r + dy - 1, c)
                index = pl.ds(start, length, stride=PITCH) if vertical else pl.ds(start, length)
                pieces.append(p_buf[slot, index, :])
            parts.append(jnp.concatenate(pieces, axis=0) if len(pieces) > 1 else pieces[0])
        return jnp.concatenate(parts, axis=1).astype(BF16)

    def update(slot, groups, c_ref, c_at):
        gates = jnp.dot(lhs_of(slot, groups), w_buf[...], preferred_element_type=F32)
        index = pl.ds(c_at, gates.shape[0])
        c_prev = c_ref[index, :]
        gi, gf, go, gg = (jnp.tanh(gates[:, hid * k:hid * (k + 1)]) for k in range(4))
        c_next = 0.5 * ((gf * c_prev + c_prev) + (gi * gg + gg))
        c_ref[index, :] = c_next
        h = (0.5 * go + 0.5) * jnp.tanh(c_next)
        at = 0
        for r, c, length, vertical in groups:
            start = cell(r, c)
            place = pl.ds(start, length, stride=PITCH) if vertical else pl.ds(start, length)
            x_buf[1 - slot, place, :] = h[at:at + length]
            at += length
        return h

    def stage_rows(slot, h_rows):
        for k, r in enumerate(edge_rows):
            row_send[slot, k, 0:cols] = h_rows[k].astype(BF16)
            row_send[slot, k, cols:2 * cols] = p_buf[slot, pl.ds(pcell(r, 0), cols), :].astype(BF16)

    def send_halo(slot, wanted):
        for d in range(8):
            @pl.when(jnp.logical_and(exists(d), wanted))
            def _():
                departure(slot, d).start()

    def receive_halo(slot):
        for d in range(8):
            @pl.when(exists(d))
            def _():
                arrival(slot, d).wait_recv()

    def unpack_halo(slot):
        for k, r in enumerate((-1, rows)):
            x_buf[slot, pl.ds(cell(r, 0), cols), :] = row_recv[slot, k, 0:cols].astype(F32)
            p_buf[slot, pl.ds(pcell(r, 0), cols), :] = row_recv[slot, k, cols:2 * cols].astype(F32)
        for k, c in enumerate((-1, cols)):
            x_buf[slot, pl.ds(cell(0, c), rows, stride=PITCH), :] = col_recv[slot, k].astype(F32)
        for k, (dr, dc) in enumerate(DIRECTIONS[4:]):
            r, pick = (-1, 15) if dr < 0 else (rows, 0)
            c = -1 if dc < 0 else cols
            x_buf[slot, pl.ds(cell(r, c), 1), :] = corner_recv[slot, k].astype(F32)[pick:pick + 1]

    def wait_sent(slot):
        for d in range(8):
            @pl.when(exists(d))
            def _():
                departure(slot, d).wait_send()

    def write_out(slot):
        for r in range(rows):
            out_buf[slot, r] = x_buf[slot, pl.ds(cell(r, 0), cols), :].astype(BF16)

    def main_rows(slot, first, last):
        update(slot, [(r, SIDE, width, False) for r in range(first, last)], c_main, (first - 1) * width)

    def one_step(t, now):
        pack_frame(jnp.minimum(t + 1, steps - 1), 1 - now)
        write_out(now)
        main_rows(now, 1, 13)
        main_rows(now, 13, 25)

        @pl.when(t >= 1)
        def _():
            out_copy(t - 1, now).start()
            wait_sent(1 - now)

        @pl.when(t >= 2)
        def _():
            out_copy(t - 2, 1 - now).wait()
        receive_halo(now)
        unpack_halo(now)

        h_col = update(now, [(0, c, rows, True) for c in edge_cols], c_col, 0)
        h_row = update(now, [(r, 0, cols, False) for r in edge_rows], c_row, 0)
        for k in range(2):
            col_send[1 - now, k] = h_col[k * rows:(k + 1) * rows].astype(BF16)
        stage_rows(1 - now, [h_row[k * cols:(k + 1) * cols] for k in range(2)])
        send_halo(1 - now, t + 1 < steps)

        update(now, [(0, c, rows, True) for c in inner_side[:SIDE - 1]], c_side, 0)
        update(now, [(0, c, rows, True) for c in inner_side[SIDE - 1:]], c_side, (SIDE - 1) * rows)
        main_rows(now, 25, 36)
        main_rows(now, 36, 47)

    frame_load(0).wait()
    for d in (2, 3):
        @pl.when(exists(d))
        def _():
            frame_side(0, d, True).wait_recv()
    pack_frame(0, 0)
    for k, c in enumerate(edge_cols):
        col_send[0, k] = x_buf[0, pl.ds(cell(0, c), rows, stride=PITCH), :].astype(BF16)
    stage_rows(0, [x_buf[0, pl.ds(cell(r, 0), cols), :] for r in edge_rows])
    send_halo(0, True)
    frame_load(1).wait()
    for d in (2, 3):
        @pl.when(exists(d))
        def _():
            frame_side(1, d, True).wait_recv()

    def two_steps(i, carry):
        one_step(2 * i, 0)
        one_step(2 * i + 1, 1)
        return carry

    lax.fori_loop(0, steps // 2, two_steps, 0)

    write_out(0)
    out_copy(steps - 1, 0).start()
    for r in range(1, rows - 1):
        cout_ref[pl.ds(r * cols + SIDE, width), :] = c_main[pl.ds((r - 1) * width, width), :]
    for i, c in enumerate(inner_side):
        cout_ref[pl.ds(c, rows, stride=cols), :] = c_side[pl.ds(i * rows, rows), :]
    for i, c in enumerate(edge_cols):
        cout_ref[pl.ds(c, rows, stride=cols), :] = c_col[pl.ds(i * rows, rows), :]
    for i, r in enumerate(edge_rows):
        cout_ref[pl.ds(r * cols, cols), :] = c_row[pl.ds(i * cols, cols), :]
    wait_sent(1)
    for part in (0, 1):
        for d in (2, 3):
            @pl.when(exists(d))
            def _():
                frame_side(part, d).wait_send()
    out_copy(steps - 2, 1).wait()
    out_copy(steps - 1, 0).wait()


def solution(mesh):
    n_rows = mesh.shape["rows"]
    n_cols = mesh.shape["cols"]
    seq_spec = P(None, "dp", "rows", "cols", None)
    state_spec = P("dp", "rows", "cols", None)

    def local_run(frames, w_in, w_rec, gate_bias, h_init, c_init):
        steps, _, rows, cols, c_in = frames.shape
        hid = h_init.shape[-1]
        vmem = pl.BlockSpec(memory_space=pltpu.VMEM)
        anywhere = pl.BlockSpec(memory_space=pl.ANY)
        seq, c_last = pl.pallas_call(
            functools.partial(kernel, steps, rows, cols, n_rows, n_cols, c_in),
            out_shape=(jax.ShapeDtypeStruct((steps, rows, cols, hid), BF16),
                       jax.ShapeDtypeStruct((rows * cols, hid), F32)),
            in_specs=[anywhere, vmem, vmem, vmem, vmem, vmem],
            out_specs=(anywhere, vmem),
            scratch_shapes=[
                pltpu.VMEM((2, (rows + 2) * PITCH, hid), F32),
                pltpu.VMEM((2, (rows + 2) * PITCH, 128), F32),
                pltpu.VMEM((9 * hid + 3 * 128, 4 * hid), BF16),
                pltpu.VMEM((steps, cols, c_in, rows), BF16),
                pltpu.VMEM((2, steps, c_in, rows), BF16),
                pltpu.VMEM(((rows - 2) * (cols - 2 * SIDE), hid), F32),
                pltpu.VMEM((rows * 2 * (SIDE - 1), hid), F32),
                pltpu.VMEM((rows * 2, hid), F32),
                pltpu.VMEM((cols * 2, hid), F32),
                pltpu.VMEM((2, rows, cols, hid), BF16),
                pltpu.VMEM((2, 2, 2 * cols, hid), BF16),
                pltpu.VMEM((2, 2, rows, hid), BF16),
                pltpu.VMEM((2, 2, 2 * cols, hid), BF16),
                pltpu.VMEM((2, 2, rows, hid), BF16),
                pltpu.VMEM((2, 4, 16, hid), BF16),
                pltpu.SemaphoreType.DMA((2, 8)),
                pltpu.SemaphoreType.DMA((2, 8)),
                pltpu.SemaphoreType.DMA((2,)),
                pltpu.SemaphoreType.DMA((2, 2)),
                pltpu.SemaphoreType.DMA((2, 2)),
                pltpu.SemaphoreType.DMA((2,)),
            ],
            compiler_params=pltpu.CompilerParams(
                collective_id=0, has_side_effects=True, vmem_limit_bytes=48 * 2**20),
            name="convlstm",
        )(jnp.transpose(frames[:, 0], (0, 2, 3, 1)), w_rec.reshape(9 * hid, 4 * hid),
          w_in.reshape(9 * c_in, 4 * hid), gate_bias.reshape(1, 4 * hid), h_init[0], c_init[0].reshape(rows * cols, hid))
        return seq[:, None], c_last.reshape(c_init.shape)

    return jax.shard_map(local_run, mesh=mesh, in_specs=(seq_spec, P(), P(), P(), state_spec, state_spec),
                         out_specs=(seq_spec, state_spec), check_vma=False)
```

time: 608 us -> 111 us (0.18); the launches traced: 599 us -> 110 us
  starting transfers between devices: 302 us -> 0 us
  matrix products: 104 us -> 0 us
  local copies, waits for them, and re-layouts: 119 us -> 15.7 us
  Pallas kernels: 0 us -> 93.9 us
  other arithmetic: 47.5 us -> 0 us
  waiting for transfers between devices: 21.5 us -> 0 us
    ppermute x100 -> x0, starting transfers between devices: 302 us -> none  [the longest x50 234 us: edge_exchange(): from_prev = lax.ppermute(high_part, axis_name, forward)]
    conv_general_dilated x48 -> x0, matrix products: 104 us -> none  [conv_valid(): lax.conv_general_dilated(operand, kernel, (1, 1), 'VALID', dimension_numb...]
    pallas_call x0 -> x1, Pallas kernels: none -> 93.9 us  [local_run(): pl.pallas_call(functools.partial(kernel, steps, rows, cols, n_rows, n_col...]
    dynamic_update_slice x24 -> x0, local copies, waits for them, and re-layouts: 23 us -> none  [local_run(): lax.scan(time_step, (h_init, c_init), frames_ext)]
    squeeze x48 -> x0, local copies, waits for them, and re-layouts: 22.9 us -> none  [local_run(): lax.scan(time_step, (h_init, c_init), frames_ext)]
    div x24 -> x0, other arithmetic: 21.5 us -> none  [cell_update(): jax.nn.sigmoid(gate_f) * c_prev + jax.nn.sigmoid(gate_i) * jnp.tanh(gate_g)]
    ppermute x100 -> x0, waiting for transfers between devices: 21.5 us -> none  [the longest x50 20 us: edge_exchange(): from_prev = lax.ppermute(high_part, axis_name, forward)]
    while x194 -> x0, local copies, waits for them, and re-layouts: 18.2 us -> none
  transfers between devices with their start and end apart: 100 -> 0, of which waited for: 26 -> 0; matrix products, arithmetic and copies ran while one was open for 8% -> 0% of each run, Pallas kernels for 0% -> 0%
where the time goes in v2:
time: 111 us; the launch traced here: 110 us
  Pallas kernels  93.9 us (85%)
  local copies, waits for them, and re-layouts  15.7 us (14%)
    pallas_call x1, Pallas kernels, local_run(): pl.pallas_call(functools.partial(kernel, steps, rows, cols, n_rows, n_col...  93.9 us
    unnamed x12, local copies, waits for them, and re-layouts  15.7 us

profile of v2, /device:TPU:0, one launch (start us, length us, event | category | flops | bytes accessed | tf_op | source)
XLA Modules:
  0.0 110.2 jit_solution(3966599482172467693)
XLA Ops:
  0.6 0.0 copy-start
  0.6 1.3 %copy-done = bf16[3,3,128,512]{3,2,1,0:T(8,128)(2,1)S(1)} copy-done((bf16[3,3,128,512]{3,2,1,0:T(8,128)(2,1)S(1)}, bf16[3,3,128,512]{3,2,1,0:T(8,128)(2,1)}, u32[]{:S(2)}) %copy-start) | copy-done | bytes 1179672
  1.9 0.0 copy-start.1
  1.9 1.1 %copy-done.1 = f32[1,48,32,128]{3,2,1,0:T(8,128)S(1)} copy-done((f32[1,48,32,128]{3,2,1,0:T(8,128)S(1)}, f32[1,48,32,128]{3,2,1,0:T(8,128)}, u32[]{:S(2)}) %copy-start.1) | copy-done | bytes 786456
  3.0 0.0 copy-start.2
  3.0 1.0 copy-done.2
  4.0 0.0 copy-start.3
  4.0 0.9 copy-done.3
  4.9 0.0 copy-start.4
  4.9 0.7 copy-done.4
  5.6 93.9 %convlstm.1 = (bf16[24,48,32,128]{3,2,1,0:T(8,128)(2,1)}, f32[1536,128]{1,0:T(8,128)S(1)}) custom-call(bf16[24,32,16,48]{3,2,1,0:T(8,128)(2,1)} %bitcast.19, bf16[1152,512]{1,0:T(8,128)(2,1)S(1)} %bitcast.12, bf16[144,512]{1,0:T(8,128)(2,1)S(1)} %bitcast.16, f32[1,512]{1,0:T(1,128)S(1)} %bitcast.17, bf16[48,32,128]{2,1,0:T(8,128)(2,1)S(1)} %bitcast.15, ...), custom_call_target="tpu_custom_call" | custom-call | tf_op jit(solution)/shard_map/convlstm/pallas_call | solution.py:318
  99.5 9.9 %copy.11 = bf16[24,1,48,32,128]{4,3,2,1,0:T(8,128)(2,1)} copy(bf16[24,1,48,32,128]{4,3,2,1,0:T(8,128)(2,1)} %bitcast.18) | data formatting | bytes 18874368
  109.4 0.9 copy.12
Async XLA Ops:
  0.6 1.3 %copy-start = (bf16[3,3,128,512]{3,2,1,0:T(8,128)(2,1)S(1)}, bf16[3,3,128,512]{3,2,1,0:T(8,128)(2,1)}, u32[]{:S(2)}) copy-start(bf16[3,3,128,512]{3,2,1,0:T(8,128)(2,1)} %param.8) | copy-start | bytes 3538948
  1.9 1.1 %copy-start.1 = (f32[1,48,32,128]{3,2,1,0:T(8,128)S(1)}, f32[1,48,32,128]{3,2,1,0:T(8,128)}, u32[]{:S(2)}) copy-start(f32[1,48,32,128]{3,2,1,0:T(8,128)} %param.11) | copy-start | bytes 2359300
  3.0 1.0 copy-start.2
  4.0 0.9 copy-start.3
  4.9 0.7 copy-start.4

commit v3 on v2

--- a/solution.py
+++ b/solution.py
@@ -14,6 +14,9 @@
 
 PITCH = 36
 DIRECTIONS = ((-1, 0), (1, 0), (0, -1), (0, 1), (-1, -1), (-1, 1), (1, -1), (1, 1))
+UNROLL = 4
+BLOCK = 10
+BESIDE = 41
 SIDE = 4
 
 
@@ -26,9 +29,9 @@
 
 
 def kernel(steps, rows, cols, n_rows, n_cols, c_in, frames_ref, w_rec_ref, w_in_ref, bias_ref, h0_ref, c0_ref,
-           seq_ref, cout_ref,
-           x_buf, p_buf, w_buf, f_buf, f_side, c_main, c_side, c_col, c_row, out_buf, row_send, col_send,
-           row_recv, col_recv, corner_recv, send_sem, recv_sem, f_sem, f_send_sem, f_recv_sem, out_sem):
+           seq_low, seq_high, cout_ref,
+           x_buf, p_buf, w_buf, bias_buf, f_buf, f_side, c_main, c_side, c_edge, row_send, col_send,
+           row_recv, col_recv, corner_recv, send_sem, recv_sem, f_sem, f_send_sem, f_recv_sem, arg_sem):
     my_row = lax.axis_index("rows")
     my_col = lax.axis_index("cols")
     hid = x_buf.shape[-1]
@@ -55,9 +58,6 @@
     def opposite(d):
         return DIRECTIONS.index((-DIRECTIONS[d][0], -DIRECTIONS[d][1]))
 
-    def out_copy(t, slot):
-        return pltpu.make_async_copy(out_buf.at[slot], seq_ref.at[t], out_sem.at[slot])
-
     def source(slot, d):
         dr, dc = DIRECTIONS[d]
         if dr and dc:
@@ -85,15 +85,26 @@
         k = d - 2
         at = k if arriving else 1 - k
         return pltpu.make_async_remote_copy(
-            src_ref=frames_ref.at[ts, edge_cols[k]], dst_ref=f_side.at[at, ts], send_sem=f_send_sem.at[part, k],
+            src_ref=f_buf.at[ts, edge_cols[k]], dst_ref=f_side.at[at, ts], send_sem=f_send_sem.at[part, k],
             recv_sem=f_recv_sem.at[part, at], device_id=device(d), device_id_type=MESH)
 
     def frame_load(part):
         ts = pl.ds(0, 1) if part == 0 else pl.ds(1, steps - 1)
         return pltpu.make_async_copy(frames_ref.at[ts], f_buf.at[ts], f_sem.at[part])
 
+    loads = [(h0_ref.at[pl.ds(0, rows // 2)], seq_low.at[steps - 1]),
+             (h0_ref.at[pl.ds(rows // 2, rows // 2)], seq_high.at[steps - 1]), (c0_ref, cout_ref), (w_rec_ref, w_buf.at[pl.ds(0, 9 * hid)]),
+             (bias_ref, bias_buf)]
+    loads += [(w_in_ref.at[pl.ds(packed * dy, packed)], w_buf.at[pl.ds(9 * hid + 128 * dy, packed)]) for dy in range(3)]
+    loads = [pltpu.make_async_copy(src, dst, arg_sem.at[k]) for k, (src, dst) in enumerate(loads)]
     frame_load(0).start()
+    for load in loads:
+        load.start()
     frame_load(1).start()
+    for slot in range(2):
+        for r in (-1, rows):
+            x_buf[slot, pl.ds(cell(r, -2), PITCH), :] = jnp.zeros((PITCH, hid), F32)
+            p_buf[slot, pl.ds(pcell(r, 0), PITCH), :] = jnp.zeros((PITCH, 128), F32)
     row_recv[...] = jnp.zeros_like(row_recv)
     col_recv[...] = jnp.zeros_like(col_recv)
     corner_recv[...] = jnp.zeros_like(corner_recv)
@@ -108,28 +119,44 @@
         count = count + exists(d).astype(jnp.int32)
     pl.semaphore_wait(barrier, count)
 
-    for part in (0, 1):
+    def send_sides(part):
+        frame_load(part).wait()
         for d in (2, 3):
             @pl.when(exists(d))
             def _():
                 frame_side(part, d).start()
 
+    def receive_sides(part):
+        for d in (2, 3):
+            @pl.when(exists(d))
+            def _():
+                frame_side(part, d, True).wait_recv()
+
+    send_sides(0)
+    for load in loads[:2]:
+        load.wait()
     for r in range(rows):
-        x_buf[0, pl.ds(cell(r, 0), cols), :] = h0_ref[r].astype(F32)
+        half, at = (seq_low, r) if r < rows // 2 else (seq_high, r - rows // 2)
+        x_buf[0, pl.ds(cell(r, 0), cols), :] = half[steps - 1, at].astype(F32)
+    loads[2].wait()
+    c_edge_at = [(c, rows, cols) for c in edge_cols] + [(r * cols, cols, 1) for r in edge_rows]
     for r in range(1, rows - 1):
-        c_main[pl.ds((r - 1) * width, width), :] = c0_ref[pl.ds(r * cols + SIDE, width), :]
+        c_main[pl.ds((r - 1) * width, width), :] = cout_ref[pl.ds(r * cols + SIDE, width), :]
     for i, c in enumerate(inner_side):
-        c_side[pl.ds(i * rows, rows), :] = c0_ref[pl.ds(c, rows, stride=cols), :]
-    for i, c in enumerate(edge_cols):
-        c_col[pl.ds(i * rows, rows), :] = c0_ref[pl.ds(c, rows, stride=cols), :]
-    for i, r in enumerate(edge_rows):
-        c_row[pl.ds(i * cols, cols), :] = c0_ref[pl.ds(r * cols, cols), :]
+        c_side[pl.ds(i * rows, rows), :] = cout_ref[pl.ds(c, rows, stride=cols), :]
+    at = 0
+    for start, length, stride in c_edge_at:
+        c_edge[pl.ds(at, length), :] = cout_ref[pl.ds(start, length, stride=stride), :]
+        at += length
+    send_sides(1)
 
     lane = lax.broadcasted_iota(jnp.int32, (1, gates_n), 1)
     scale = jnp.where(lane < 3 * hid, 0.5, 1.0)
+    for load in loads[3:]:
+        load.wait()
     for at in range(0, 9 * hid, 128):
-        w_buf[pl.ds(at, 128), :] = (w_rec_ref[pl.ds(at, 128), :].astype(F32) * scale).astype(BF16)
-    bias = bias_ref[...] * scale
+        w_buf[pl.ds(at, 128), :] = (w_buf[pl.ds(at, 128), :].astype(F32) * scale).astype(BF16)
+    bias = bias_buf[...] * scale
     b0 = bias.astype(BF16).astype(F32)
     b1 = (bias - b0).astype(BF16).astype(F32)
     b2 = bias - b0 - b1
@@ -137,7 +164,7 @@
     bias_rows = jnp.where(row == 0, b0, jnp.where(row == 1, b1, jnp.where(row == 2, b2, 0.0)))
     for dy in range(3):
         at = 9 * hid + 128 * dy
-        w_buf[pl.ds(at, packed), :] = (w_in_ref[pl.ds(packed * dy, packed), :].astype(F32) * scale).astype(BF16)
+        w_buf[pl.ds(at, packed), :] = (w_buf[pl.ds(at, packed), :].astype(F32) * scale).astype(BF16)
         w_buf[pl.ds(at + packed, 128 - packed), :] = jnp.zeros((128 - packed, gates_n), BF16)
         if dy == 1:
             w_buf[pl.ds(at + packed, 16), :] = bias_rows.astype(BF16)
@@ -175,8 +202,10 @@
             parts.append(jnp.concatenate(pieces, axis=0) if len(pieces) > 1 else pieces[0])
         return jnp.concatenate(parts, axis=1).astype(BF16)
 
-    def update(slot, groups, c_ref, c_at):
-        gates = jnp.dot(lhs_of(slot, groups), w_buf[...], preferred_element_type=F32)
+    def gates_of(slot, groups):
+        return jnp.dot(lhs_of(slot, groups), w_buf[...], preferred_element_type=F32)
+
+    def finish(slot, groups, gates, c_ref, c_at):
         index = pl.ds(c_at, gates.shape[0])
         c_prev = c_ref[index, :]
         gi, gf, go, gg = (jnp.tanh(gates[:, hid * k:hid * (k + 1)]) for k in range(4))
@@ -191,6 +220,9 @@
             at += length
         return h
 
+    def update(slot, groups, c_ref, c_at):
+        return finish(slot, groups, gates_of(slot, groups), c_ref, c_at)
+
     def stage_rows(slot, h_rows):
         for k, r in enumerate(edge_rows):
             row_send[slot, k, 0:cols] = h_rows[k].astype(BF16)
@@ -225,83 +257,72 @@
             def _():
                 departure(slot, d).wait_send()
 
-    def write_out(slot):
+    def write_out(t, slot):
         for r in range(rows):
-            out_buf[slot, r] = x_buf[slot, pl.ds(cell(r, 0), cols), :].astype(BF16)
+            half, at = (seq_low, r) if r < rows // 2 else (seq_high, r - rows // 2)
+            half[t, at] = x_buf[slot, pl.ds(cell(r, 0), cols), :].astype(BF16)
+
+    def run_of(first, last):
+        return [(r, SIDE, width, False) for r in range(first, last)]
 
     def main_rows(slot, first, last):
-        update(slot, [(r, SIDE, width, False) for r in range(first, last)], c_main, (first - 1) * width)
+        update(slot, run_of(first, last), c_main, (first - 1) * width)
+
+    edge_groups = [(0, c, rows, True) for c in edge_cols] + [(r, 0, cols, False) for r in edge_rows]
 
     def one_step(t, now):
         pack_frame(jnp.minimum(t + 1, steps - 1), 1 - now)
-        write_out(now)
-        main_rows(now, 1, 13)
-        main_rows(now, 13, 25)
+        write_out(jnp.maximum(t - 1, 0), now)
+        for at in range(1, BESIDE, BLOCK):
+            main_rows(now, at, min(at + BLOCK, BESIDE))
+        update(now, [(0, c, rows, True) for c in inner_side[:SIDE - 1]], c_side, 0)
+        update(now, [(0, c, rows, True) for c in inner_side[SIDE - 1:]], c_side, (SIDE - 1) * rows)
 
         @pl.when(t >= 1)
         def _():
-            out_copy(t - 1, now).start()
             wait_sent(1 - now)
-
-        @pl.when(t >= 2)
-        def _():
-            out_copy(t - 2, 1 - now).wait()
         receive_halo(now)
         unpack_halo(now)
 
-        h_col = update(now, [(0, c, rows, True) for c in edge_cols], c_col, 0)
-        h_row = update(now, [(r, 0, cols, False) for r in edge_rows], c_row, 0)
+        edge_gates = gates_of(now, edge_groups)
+        gates = gates_of(now, run_of(BESIDE, rows - 1))
+        h = finish(now, edge_groups, edge_gates, c_edge, 0)
         for k in range(2):
-            col_send[1 - now, k] = h_col[k * rows:(k + 1) * rows].astype(BF16)
-        stage_rows(1 - now, [h_row[k * cols:(k + 1) * cols] for k in range(2)])
+            col_send[1 - now, k] = h[k * rows:(k + 1) * rows].astype(BF16)
+        stage_rows(1 - now, [h[2 * rows + k * cols:2 * rows + (k + 1) * cols] for k in range(2)])
         send_halo(1 - now, t + 1 < steps)
-
-        update(now, [(0, c, rows, True) for c in inner_side[:SIDE - 1]], c_side, 0)
-        update(now, [(0, c, rows, True) for c in inner_side[SIDE - 1:]], c_side, (SIDE - 1) * rows)
-        main_rows(now, 25, 36)
-        main_rows(now, 36, 47)
-
-    frame_load(0).wait()
-    for d in (2, 3):
-        @pl.when(exists(d))
-        def _():
-            frame_side(0, d, True).wait_recv()
+        finish(now, run_of(BESIDE, rows - 1), gates, c_main, (BESIDE - 1) * width)
+
+    receive_sides(0)
     pack_frame(0, 0)
     for k, c in enumerate(edge_cols):
         col_send[0, k] = x_buf[0, pl.ds(cell(0, c), rows, stride=PITCH), :].astype(BF16)
     stage_rows(0, [x_buf[0, pl.ds(cell(r, 0), cols), :] for r in edge_rows])
     send_halo(0, True)
-    frame_load(1).wait()
-    for d in (2, 3):
-        @pl.when(exists(d))
-        def _():
-            frame_side(1, d, True).wait_recv()
-
-    def two_steps(i, carry):
-        one_step(2 * i, 0)
-        one_step(2 * i + 1, 1)
+    receive_sides(1)
+
+    def trip(i, carry):
+        for k in range(UNROLL):
+            one_step(UNROLL * i + k, k % 2)
         return carry
 
-    lax.fori_loop(0, steps // 2, two_steps, 0)
-
-    write_out(0)
-    out_copy(steps - 1, 0).start()
+    lax.fori_loop(0, steps // UNROLL, trip, 0)
+
+    write_out(steps - 1, 0)
     for r in range(1, rows - 1):
         cout_ref[pl.ds(r * cols + SIDE, width), :] = c_main[pl.ds((r - 1) * width, width), :]
     for i, c in enumerate(inner_side):
         cout_ref[pl.ds(c, rows, stride=cols), :] = c_side[pl.ds(i * rows, rows), :]
-    for i, c in enumerate(edge_cols):
-        cout_ref[pl.ds(c, rows, stride=cols), :] = c_col[pl.ds(i * rows, rows), :]
-    for i, r in enumerate(edge_rows):
-        cout_ref[pl.ds(r * cols, cols), :] = c_row[pl.ds(i * cols, cols), :]
+    at = 0
+    for start, length, stride in c_edge_at:
+        cout_ref[pl.ds(start, length, stride=stride), :] = c_edge[pl.ds(at, length), :]
+        at += length
     wait_sent(1)
     for part in (0, 1):
         for d in (2, 3):
             @pl.when(exists(d))
             def _():
                 frame_side(part, d).wait_send()
-    out_copy(steps - 2, 1).wait()
-    out_copy(steps - 1, 0).wait()
 
 
 def solution(mesh):
@@ -314,24 +335,26 @@
         steps, _, rows, cols, c_in = frames.shape
         hid = h_init.shape[-1]
         vmem = pl.BlockSpec(memory_space=pltpu.VMEM)
-        anywhere = pl.BlockSpec(memory_space=pl.ANY)
-        seq, c_last = pl.pallas_call(
+        args = (jnp.transpose(frames[:, 0], (0, 2, 3, 1)), w_rec.reshape(9 * hid, 4 * hid),
+                w_in.reshape(9 * c_in, 4 * hid), gate_bias.reshape(1, 4 * hid), h_init[0],
+                c_init[0].reshape(rows * cols, hid))
+        hbm = pl.BlockSpec(memory_space=pltpu.HBM)
+        low, high, c_last = pl.pallas_call(
             functools.partial(kernel, steps, rows, cols, n_rows, n_cols, c_in),
-            out_shape=(jax.ShapeDtypeStruct((steps, rows, cols, hid), BF16),
-                       jax.ShapeDtypeStruct((rows * cols, hid), F32)),
-            in_specs=[anywhere, vmem, vmem, vmem, vmem, vmem],
-            out_specs=(anywhere, vmem),
+            out_shape=(jax.ShapeDtypeStruct((steps, rows // 2, cols, hid), BF16),) * 2 + (
+                jax.ShapeDtypeStruct((rows * cols, hid), F32),),
+            in_specs=[hbm] * 6,
+            out_specs=(vmem,) * 3,
             scratch_shapes=[
                 pltpu.VMEM((2, (rows + 2) * PITCH, hid), F32),
                 pltpu.VMEM((2, (rows + 2) * PITCH, 128), F32),
                 pltpu.VMEM((9 * hid + 3 * 128, 4 * hid), BF16),
+                pltpu.VMEM((1, 4 * hid), F32),
                 pltpu.VMEM((steps, cols, c_in, rows), BF16),
                 pltpu.VMEM((2, steps, c_in, rows), BF16),
                 pltpu.VMEM(((rows - 2) * (cols - 2 * SIDE), hid), F32),
                 pltpu.VMEM((rows * 2 * (SIDE - 1), hid), F32),
-                pltpu.VMEM((rows * 2, hid), F32),
-                pltpu.VMEM((cols * 2, hid), F32),
-                pltpu.VMEM((2, rows, cols, hid), BF16),
+                pltpu.VMEM(((rows + cols) * 2, hid), F32),
                 pltpu.VMEM((2, 2, 2 * cols, hid), BF16),
                 pltpu.VMEM((2, 2, rows, hid), BF16),
                 pltpu.VMEM((2, 2, 2 * cols, hid), BF16),
@@ -342,13 +365,13 @@
                 pltpu.SemaphoreType.DMA((2,)),
                 pltpu.SemaphoreType.DMA((2, 2)),
                 pltpu.SemaphoreType.DMA((2, 2)),
-                pltpu.SemaphoreType.DMA((2,)),
+                pltpu.SemaphoreType.DMA((8,)),
             ],
             compiler_params=pltpu.CompilerParams(
-                collective_id=0, has_side_effects=True, vmem_limit_bytes=48 * 2**20),
+                collective_id=0, has_side_effects=True, vmem_limit_bytes=24 * 2**20),
             name="convlstm",
-        )(jnp.transpose(frames[:, 0], (0, 2, 3, 1)), w_rec.reshape(9 * hid, 4 * hid),
-          w_in.reshape(9 * c_in, 4 * hid), gate_bias.reshape(1, 4 * hid), h_init[0], c_init[0].reshape(rows * cols, hid))
+        )(*(pltpu.with_memory_space_constraint(x, pltpu.HBM) for x in args))
+        seq = jnp.concatenate([low, high], axis=1)
         return seq[:, None], c_last.reshape(c_init.shape)
 
     return jax.shard_map(local_run, mesh=mesh, in_specs=(seq_spec, P(), P(), P(), state_spec, state_spec),

time: 111 us -> 95.2 us (0.86)
  local copies, waits for them, and re-layouts: 15.7 us -> 0.88 us
  Pallas kernels: 93.9 us -> 89.3 us
  other arithmetic: 0 us -> 4.02 us
    unnamed x12 -> x1, local copies, waits for them, and re-layouts: 15.7 us -> 0.88 us
    pallas_call x1, Pallas kernels: 93.9 us -> 89.3 us  [local_run(): pl.pallas_call(functools.partial(kernel, steps, rows, cols, n_rows, n_col...]
    unnamed x0 -> x1, other arithmetic: none -> 4.02 us
where the time goes in v3:
time: 95.2 us; the launch traced here: 94.8 us
  Pallas kernels  89.3 us (94%)
  other arithmetic  4.02 us (4%)
    pallas_call x1, Pallas kernels, local_run(): pl.pallas_call(functools.partial(kernel, steps, rows, cols, n_rows, n_col...  89.3 us
    unnamed x1, other arithmetic  4.02 us

profile of v3, /device:TPU:0, one launch (start us, length us, event | category | flops | bytes accessed | tf_op | source)
XLA Modules:
  0.0 94.8 jit_solution(3968793296609020572)
XLA Ops:
  0.6 89.3 %convlstm.1 = (bf16[24,24,32,128]{3,2,1,0:T(8,128)(2,1)S(1)}, bf16[24,24,32,128]{3,2,1,0:T(8,128)(2,1)S(1)}, f32[1536,128]{1,0:T(8,128)S(1)}) custom-call(bf16[24,32,16,48]{3,2,1,0:T(8,128)(2,1)} %bitcast.14, bf16[1152,512]{1,0:T(8,128)(2,1)} %bitcast.15, bf16[144,512]{1,0:T(8,128)(2,1)} %bitcast.18, f32[1,512]{1,0:T(1,128)} %bitcast.19, ...), custom_call_target="tpu_custom_call" | custom-call | tf_op jit(solution)/shard_map/convlstm/pallas_call | solution.py:342
  89.9 4.0 %maximum_bitcast_fusion = bf16[24,1,48,32,128]{4,3,2,1,0:T(8,128)(2,1)} fusion(bf16[24,24,32,128]{3,2,1,0:T(8,128)(2,1)S(1)} %get-tuple-element.6, bf16[24,24,32,128]{3,2,1,0:T(8,128)(2,1)S(1)} %get-tuple-element.5), kind=kLoop, calls=%fused_computation | loop fusion | flops 4718592 | bytes 18874368
  93.9 0.9 copy.10

commit v4 on v3

v4 whole, which is shorter than its diff:
```python
import functools

import jax
import jax.numpy as jnp
from jax import lax
from jax.experimental import pallas as pl
from jax.experimental.pallas import tpu as pltpu
from jax.sharding import PartitionSpec as P

MESH = pl.DeviceIdType.MESH
BF16 = jnp.bfloat16
F32 = jnp.float32
TDT = jnp.bfloat16

PITCH = 36
DIRECTIONS = ((-1, 0), (1, 0), (0, -1), (0, 1), (-1, -1), (-1, 1), (1, -1), (1, 1))
BLOCK = 11
SIDE = 4


def cell(r, c):
    return (r + 2) * PITCH + c + 2


def pcell(r, c):
    return (r + 2) * PITCH + c + 1


def kernel(steps, rows, cols, n_rows, n_cols, c_in, frames_ref, w_rec_ref, w_in_ref, bias_ref, h0_ref, c0_ref,
           seq_low, seq_high, cout_ref,
           x_buf, p_buf, w_buf, bias_buf, f_buf, f_side, c_main, c_col, c_row, ring_row, ring_col,
           row_send, col_send, crow_send, ccol_send,
           row_recv, col_recv, corner_recv, crow_recv, ccol_recv, ccorner_recv,
           send_sem, recv_sem, f_sem, f_send_sem, f_recv_sem, arg_sem):
    my_row = lax.axis_index("rows")
    my_col = lax.axis_index("cols")
    hid = x_buf.shape[-1]
    gates_n = 4 * hid
    packed = 3 * c_in
    width = cols - 2 * SIDE
    half = rows // 2
    long = rows + 8
    side_cols = tuple(range(SIDE)) + tuple(range(cols - SIDE, cols))
    edge_rows = (0, 1, rows - 2, rows - 1)

    def exists(d):
        dr, dc = DIRECTIONS[d]
        ok = None
        for here, step, count in ((my_row, dr, n_rows), (my_col, dc, n_cols)):
            if step:
                this = (here > 0) if step < 0 else (here < count - 1)
                ok = this if ok is None else jnp.logical_and(ok, this)
        return ok

    def device(d):
        dr, dc = DIRECTIONS[d]
        return {"rows": my_row + dr, "cols": my_col + dc}

    def opposite(d):
        return DIRECTIONS.index((-DIRECTIONS[d][0], -DIRECTIONS[d][1]))

    def source(slot, d, kind):
        dr, dc = DIRECTIONS[d]
        if dr and dc:
            k = 0 if dc < 0 else 1
            if kind:
                return ccol_send.at[slot, k, pl.ds(0 if dr < 0 else rows - 8, 8)]
            return col_send.at[slot, k, :, pl.ds(0 if dr < 0 else rows - 16, 16)]
        if dr:
            return (crow_send if kind else row_send).at[slot, d]
        return (ccol_send if kind else col_send).at[slot, d - 2]

    def landing(slot, d, kind):
        dr, dc = DIRECTIONS[d]
        if dr and dc:
            return (ccorner_recv if kind else corner_recv).at[slot, d - 4]
        if dr:
            return (crow_recv if kind else row_recv).at[slot, d]
        return (ccol_recv if kind else col_recv).at[slot, d - 2]

    def departure(slot, d, kind):
        return pltpu.make_async_remote_copy(
            src_ref=source(slot, d, kind), dst_ref=landing(slot, opposite(d), kind), send_sem=send_sem.at[slot, kind, d],
            recv_sem=recv_sem.at[slot, kind, opposite(d)], device_id=device(d), device_id_type=MESH)

    def arrival(slot, d, kind):
        return pltpu.make_async_remote_copy(
            src_ref=source(slot, d, kind), dst_ref=landing(slot, d, kind), send_sem=send_sem.at[slot, kind, d],
            recv_sem=recv_sem.at[slot, kind, d], device_id=device(d), device_id_type=MESH)

    def frame_part(part):
        return pl.ds(0, 2) if part == 0 else pl.ds(2, steps - 2)

    def frame_side(part, d, arriving=False):
        ts = frame_part(part)
        k = d - 2
        at = k if arriving else 1 - k
        return pltpu.make_async_remote_copy(
            src_ref=f_buf.at[ts, pl.ds(0 if k == 0 else cols - 2, 2)], dst_ref=f_side.at[at, ts],
            send_sem=f_send_sem.at[part, k], recv_sem=f_recv_sem.at[part, at], device_id=device(d), device_id_type=MESH)

    def frame_load(part):
        ts = frame_part(part)
        return pltpu.make_async_copy(frames_ref.at[ts], f_buf.at[ts], f_sem.at[part])

    loads = [(h0_ref.at[pl.ds(0, half)], seq_low.at[steps - 1]), (h0_ref.at[pl.ds(half, half)], seq_high.at[steps - 1]),
             (c0_ref, cout_ref), (w_rec_ref, w_buf.at[pl.ds(0, 9 * hid)]), (bias_ref, bias_buf)]
    loads += [(w_in_ref.at[pl.ds(packed * dy, packed)], w_buf.at[pl.ds(9 * hid + 128 * dy, packed)]) for dy in range(3)]
    loads = [pltpu.make_async_copy(src, dst, arg_sem.at[k]) for k, (src, dst) in enumerate(loads)]
    frame_load(0).start()
    for load in loads:
        load.start()
    frame_load(1).start()
    for ref in (row_recv, col_recv, corner_recv, crow_recv, ccol_recv, ccorner_recv, f_side):
        ref[...] = jnp.zeros_like(ref)
    for slot in range(2):
        x_buf[slot, pl.ds(0, 2 * PITCH), :] = jnp.zeros((2 * PITCH, hid), F32)
        x_buf[slot, pl.ds((rows + 2) * PITCH, 10 * PITCH), :] = jnp.zeros((10 * PITCH, hid), F32)
    for slot in range(4):
        p_buf[slot, pl.ds(0, 2 * PITCH), :] = jnp.zeros((2 * PITCH, 128), F32)
        p_buf[slot, pl.ds((rows + 2) * PITCH, 10 * PITCH), :] = jnp.zeros((10 * PITCH, 128), F32)
    ring_col[...] = jnp.zeros_like(ring_col)

    barrier = pltpu.get_barrier_semaphore()
    count = jnp.int32(0)
    for d in range(8):
        @pl.when(exists(d))
        def _():
            pl.semaphore_signal(barrier, inc=1, device_id=device(d), device_id_type=MESH)
        count = count + exists(d).astype(jnp.int32)
    pl.semaphore_wait(barrier, count)

    def send_sides(part):
        frame_load(part).wait()
        for d in (2, 3):
            @pl.when(exists(d))
            def _():
                frame_side(part, d).start()

    def receive_sides(part):
        for d in (2, 3):
            @pl.when(exists(d))
            def _():
                frame_side(part, d, True).wait_recv()

    send_sides(0)
    for load in loads[:2]:
        load.wait()
    for r in range(rows):
        part, at = (seq_low, r) if r < half else (seq_high, r - half)
        x_buf[0, pl.ds(cell(r, 0), cols), :] = part[steps - 1, at].astype(F32)
    loads[2].wait()
    for r in range(2, rows - 2):
        c_main[pl.ds((r - 2) * width, width), :] = cout_ref[pl.ds(r * cols + SIDE, width), :]
    for i, c in enumerate(side_cols):
        c_col[pl.ds(i * rows, rows), :] = cout_ref[pl.ds(c, rows, stride=cols), :]
    for i, r in enumerate(edge_rows):
        c_row[pl.ds(i * cols, cols), :] = cout_ref[pl.ds(r * cols, cols), :]
    send_sides(1)

    lane = lax.broadcasted_iota(jnp.int32, (1, gates_n), 1)
    scale = jnp.where(lane < 3 * hid, 0.5, 1.0)
    for load in loads[3:]:
        load.wait()
    for at in range(0, 9 * hid, 128):
        w_buf[pl.ds(at, 128), :] = (w_buf[pl.ds(at, 128), :].astype(F32) * scale).astype(BF16)
    bias = bias_buf[...] * scale
    b0 = bias.astype(BF16).astype(F32)
    b1 = (bias - b0).astype(BF16).astype(F32)
    b2 = bias - b0 - b1
    row = lax.broadcasted_iota(jnp.int32, (16, gates_n), 0)
    bias_rows = jnp.where(row == 0, b0, jnp.where(row == 1, b1, jnp.where(row == 2, b2, 0.0)))
    for dy in range(3):
        at = 9 * hid + 128 * dy
        w_buf[pl.ds(at, packed), :] = (w_buf[pl.ds(at, packed), :].astype(F32) * scale).astype(BF16)
        w_buf[pl.ds(at + packed, 128 - packed), :] = jnp.zeros((128 - packed, gates_n), BF16)
        if dy == 1:
            w_buf[pl.ds(at + packed, 16), :] = bias_rows.astype(BF16)

    row = lax.broadcasted_iota(jnp.int32, (128 - packed, rows), 0)
    ones = jnp.where(row < 3, 1.0, 0.0).astype(BF16)

    def pack_frame(t, slot):
        for c in range(-1, cols + 1):
            pieces = []
            for k in range(c - 1, c + 2):
                if k < 0:
                    pieces.append(f_side[0, t, k + 2])
                elif k < cols:
                    pieces.append(f_buf[t, k])
                else:
                    pieces.append(f_side[1, t, k - cols])
            window = jnp.concatenate(pieces + [ones], axis=0)
            p_buf[slot, pl.ds(pcell(0, c), rows, stride=PITCH), :] = window.T.astype(F32)

    def run_index(start, length, vertical):
        return pl.ds(start, length, stride=PITCH) if vertical else pl.ds(start, length)

    def gates_of(slot, p_slot, groups):
        parts = []
        for dy in range(3):
            for dx in range(3):
                pieces = [x_buf[slot, run_index(cell(r + dy - 1, c + dx - 1), length, vertical), :]
                          for r, c, length, vertical in groups]
                parts.append(jnp.concatenate(pieces, axis=0) if len(pieces) > 1 else pieces[0])
        for dy in range(3):
            pieces = [p_buf[p_slot, run_index(pcell(r + dy - 1, c), length, vertical), :]
                      for r, c, length, vertical in groups]
            parts.append(jnp.concatenate(pieces, axis=0) if len(pieces) > 1 else pieces[0])
        lhs = jnp.concatenate(parts, axis=1).astype(BF16)
        return jnp.dot(lhs, w_buf[...], preferred_element_type=F32)

    def finish(slot, groups, gates, c_ref, c_at, mask=None):
        index = pl.ds(c_at, gates.shape[0])
        c_prev = c_ref[index, :]
        gi, gf, go, gg = (jnp.tanh(gates[:, hid * k:hid * (k + 1)]) for k in range(4))
        c_next = 0.5 * ((gf * c_prev + c_prev) + (gi * gg + gg))
        h = (0.5 * go + 0.5) * jnp.tanh(c_next)
        if mask is None:
            c_ref[index, :] = c_next
        else:
            h = h * mask
        at = 0
        for r, c, length, vertical in groups:
            x_buf[1 - slot, run_index(cell(r, c), length, vertical), :] = h[at:at + length]
            at += length

    def update(slot, p_slot, groups, c_ref, c_at):
        finish(slot, groups, gates_of(slot, p_slot, groups), c_ref, c_at)

    def stage(slot, p_first):
        state = x_buf.at[0]
        for k, r in enumerate((0, rows - 2)):
            for n in range(2):
                row_send[slot, k, n * cols:(n + 1) * cols] = state[pl.ds(cell(r + n, 0), cols), :].astype(BF16)
            at = 2 * cols
            row_send[slot, k, at:at + 2 * PITCH] = p_buf[p_first, pl.ds(pcell(r, -1), 2 * PITCH), :].astype(BF16)
            at += 2 * PITCH
            r_one = 0 if k == 0 else rows - 1
            row_send[slot, k, at:at + PITCH] = p_buf[p_first + 1, pl.ds(pcell(r_one, -1), PITCH), :].astype(BF16)
            crow_send[slot, k] = c_row[pl.ds((0 if k == 0 else 3) * cols, cols), :]
        for k, c in enumerate((0, cols - 2)):
            for n in range(2):
                col_send[slot, k, n] = state[pl.ds(cell(0, c + n), rows, stride=PITCH), :].astype(BF16)
            ccol_send[slot, k] = c_col[pl.ds((0 if k == 0 else 2 * SIDE - 1) * rows, rows), :]

    def send_halo(slot, wanted):
        for d in range(8):
            @pl.when(jnp.logical_and(exists(d), wanted))
            def _():
                departure(slot, d, 0).start()
                departure(slot, d, 1).start()

    def receive_halo(slot):
        for d in range(8):
            @pl.when(exists(d))
            def _():
                arrival(slot, d, 0).wait_recv()
                arrival(slot, d, 1).wait_recv()

    def unpack_halo(slot, p_first):
        state = x_buf.at[0]
        for k, r in enumerate((-2, rows)):
            for n in range(2):
                state[pl.ds(cell(r + n, 0), cols), :] = row_recv[slot, k, n * cols:(n + 1) * cols].astype(F32)
            at = 2 * cols
            p_buf[p_first, pl.ds(pcell(r, -1), 2 * PITCH), :] = row_recv[slot, k, at:at + 2 * PITCH].astype(F32)
            at += 2 * PITCH
            r_one = -1 if k == 0 else rows
            p_buf[p_first + 1, pl.ds(pcell(r_one, -1), PITCH), :] = row_recv[slot, k, at:at + PITCH].astype(F32)
            ring_row[pl.ds(k * cols, cols), :] = crow_recv[slot, k]
        for k, c in enumerate((-2, cols)):
            for n in range(2):
                state[pl.ds(cell(0, c + n), rows, stride=PITCH), :] = col_recv[slot, k, n].astype(F32)
            ring_col[pl.ds(k * long + 1, rows), :] = ccol_recv[slot, k]
        for k, (dr, dc) in enumerate(DIRECTIONS[4:]):
            r, pick = (-2, 14) if dr < 0 else (rows, 0)
            c = -2 if dc < 0 else cols
            for n in range(2):
                state[pl.ds(cell(r, c + n), 2, stride=PITCH), :] = corner_recv[slot, k, n].astype(F32)[pick:pick + 2]
            at = (0 if dc < 0 else long) + (0 if dr < 0 else rows + 1)
            pick = 7 if dr < 0 else 0
            ring_col[pl.ds(at, 1), :] = ccorner_recv[slot, k][pick:pick + 1]

    def wait_sent(slot):
        for d in range(8):
            @pl.when(exists(d))
            def _():
                departure(slot, d, 0).wait_send()
                departure(slot, d, 1).wait_send()

    def write_out(t, slot):
        for r in range(rows):
            part, at = (seq_low, r) if r < half else (seq_high, r - half)
            part[t, at] = x_buf[slot, pl.ds(cell(r, 0), cols), :].astype(BF16)

    def main_run(first, last):
        return [(r, SIDE, width, False) for r in range(first, last)]

    def main_rows(slot, p_slot, first, last):
        update(slot, p_slot, main_run(first, last), c_main, (first - 2) * width)

    def side_run(*ids):
        return [(0, side_cols[i], rows, True) for i in ids]

    there = [jnp.where(exists(d), 1.0, 0.0).astype(F32) for d in range(4)]
    place = lax.broadcasted_iota(jnp.int32, (long, hid), 0)
    ends = jnp.where(place == 0, there[0], jnp.where(place == rows + 1, there[1], 1.0))
    ring_mask = jnp.concatenate([ends * there[2], ends * there[3],
                                 jnp.full((cols, hid), 1.0, F32) * there[0], jnp.full((cols, hid), 1.0, F32) * there[1]],
                                axis=0)
    ring_col_run = [(-1, -1, long, True), (-1, cols, long, True)]
    ring_row_run = [(-1, 0, cols, False), (rows, 0, cols, False)]
    row_run = [(r, 0, cols, False) for r in edge_rows]
    n_long = 2 * long
    last = 2 * SIDE - 1

    def pair(m, now):
        t = 2 * m
        pa = 2 * now
        other = 2 * (1 - now)
        pack_frame(jnp.minimum(t + 2, steps - 2), other)
        pack_frame(jnp.minimum(t + 3, steps - 1), other + 1)
        write_out(jnp.maximum(t - 1, 0), 0)
        for at in range(2, rows - 2, BLOCK):
            main_rows(0, pa, at, at + BLOCK)
        update(0, pa, side_run(1, 2, 3), c_col, rows)
        update(0, pa, side_run(last - 3, last - 2, last - 1), c_col, (last - 3) * rows)

        @pl.when(m >= 1)
        def _():
            wait_sent(1 - now)
        receive_halo(now)
        unpack_halo(now, pa)

        own = side_run(0) + side_run(last) + row_run
        own_gates = gates_of(0, pa, own)
        ring_gates = gates_of(0, pa, ring_col_run + ring_row_run)
        beside = gates_of(1, pa + 1, main_run(13, 21))
        finish(0, side_run(0), own_gates[:rows], c_col, 0)
        finish(0, side_run(last), own_gates[rows:2 * rows], c_col, last * rows)
        finish(0, row_run, own_gates[2 * rows:], c_row, 0)
        finish(0, ring_col_run, ring_gates[:n_long], ring_col, 0, ring_mask[:n_long])
        finish(0, ring_row_run, ring_gates[n_long:], ring_row, 0, ring_mask[n_long:])
        for i, r in ((0, 0), (3, rows - 1)):
            for first in (1, last - 3):
                c_col[pl.ds(first * rows + r, 3, stride=rows), :] = c_row[pl.ds(i * cols + side_cols[first], 3), :]
        finish(1, main_run(13, 21), beside, c_main, (13 - 2) * width)
        left = side_run(0, 1) + side_run(last - 1, last)
        edge_gates = gates_of(1, pa + 1, left + row_run)
        beside = gates_of(1, pa + 1, main_run(21, 29))
        finish(1, side_run(0, 1), edge_gates[:2 * rows], c_col, 0)
        finish(1, side_run(last - 1, last), edge_gates[2 * rows:4 * rows], c_col, (last - 1) * rows)
        finish(1, row_run, edge_gates[4 * rows:], c_row, 0)
        stage(1 - now, other)
        send_halo(1 - now, t + 2 < steps)

        finish(1, main_run(21, 29), beside, c_main, (21 - 2) * width)
        write_out(t, 1)
        main_rows(1, pa + 1, 2, 13)
        main_rows(1, pa + 1, 29, 38)
        main_rows(1, pa + 1, 38, 46)
        update(1, pa + 1, side_run(2, 3), c_col, 2 * rows)
        update(1, pa + 1, side_run(last - 3, last - 2), c_col, (last - 3) * rows)

    receive_sides(0)
    pack_frame(0, 0)
    pack_frame(1, 1)
    stage(0, 0)
    send_halo(0, True)
    receive_sides(1)

    def trip(i, carry):
        pair(2 * i, 0)
        pair(2 * i + 1, 1)
        return carry

    lax.fori_loop(0, steps // 4, trip, 0)

    write_out(steps - 1, 0)
    for r in range(2, rows - 2):
        cout_ref[pl.ds(r * cols + SIDE, width), :] = c_main[pl.ds((r - 2) * width, width), :]
    for i, c in enumerate(side_cols):
        cout_ref[pl.ds(c, rows, stride=cols), :] = c_col[pl.ds(i * rows, rows), :]
    for i, r in enumerate(edge_rows):
        cout_ref[pl.ds(r * cols, cols), :] = c_row[pl.ds(i * cols, cols), :]
    wait_sent(1)
    for part in (0, 1):
        for d in (2, 3):
            @pl.when(exists(d))
            def _():
                frame_side(part, d).wait_send()


def solution(mesh):
    n_rows = mesh.shape["rows"]
    n_cols = mesh.shape["cols"]
    seq_spec = P(None, "dp", "rows", "cols", None)
    state_spec = P("dp", "rows", "cols", None)

    def local_run(frames, w_in, w_rec, gate_bias, h_init, c_init):
        steps, _, rows, cols, c_in = frames.shape
        hid = h_init.shape[-1]
        row_words = 2 * cols + 3 * PITCH + 4
        vmem = pl.BlockSpec(memory_space=pltpu.VMEM)
        args = (jnp.transpose(frames[:, 0], (0, 2, 3, 1)), w_rec.reshape(9 * hid, 4 * hid),
                w_in.reshape(9 * c_in, 4 * hid), gate_bias.reshape(1, 4 * hid), h_init[0],
                c_init[0].reshape(rows * cols, hid))
        hbm = pl.BlockSpec(memory_space=pltpu.HBM)
        low, high, c_last = pl.pallas_call(
            functools.partial(kernel, steps, rows, cols, n_rows, n_cols, c_in),
            out_shape=(jax.ShapeDtypeStruct((steps, rows // 2, cols, hid), BF16),) * 2 + (
                jax.ShapeDtypeStruct((rows * cols, hid), F32),),
            in_specs=[hbm] * 6,
            out_specs=(vmem,) * 3,
            scratch_shapes=[
                pltpu.VMEM((2, (rows + 12) * PITCH, hid), F32),
                pltpu.VMEM((4, (rows + 12) * PITCH, 128), F32),
                pltpu.VMEM((9 * hid + 3 * 128, 4 * hid), BF16),
                pltpu.VMEM((1, 4 * hid), F32),
                pltpu.VMEM((steps, cols, c_in, rows), BF16),
                pltpu.VMEM((2, steps, 2, c_in, rows), BF16),
                pltpu.VMEM(((rows - 4) * (cols - 2 * SIDE), hid), F32),
                pltpu.VMEM((rows * 2 * SIDE, hid), F32),
                pltpu.VMEM((cols * 4, hid), F32),
                pltpu.VMEM((cols * 2, hid), F32),
                pltpu.VMEM(((rows + 8) * 2, hid), F32),
                pltpu.VMEM((2, 2, row_words, hid), BF16),
                pltpu.VMEM((2, 2, 2, rows, hid), BF16),
                pltpu.VMEM((2, 2, cols, hid), F32),
                pltpu.VMEM((2, 2, rows, hid), F32),
                pltpu.VMEM((2, 2, row_words, hid), BF16),
                pltpu.VMEM((2, 2, 2, rows, hid), BF16),
                pltpu.VMEM((2, 4, 2, 16, hid), BF16),
                pltpu.VMEM((2, 2, cols, hid), F32),
                pltpu.VMEM((2, 2, rows, hid), F32),
                pltpu.VMEM((2, 4, 8, hid), F32),
                pltpu.SemaphoreType.DMA((2, 2, 8)),
                pltpu.SemaphoreType.DMA((2, 2, 8)),
                pltpu.SemaphoreType.DMA((2,)),
                pltpu.SemaphoreType.DMA((2, 2)),
                pltpu.SemaphoreType.DMA((2, 2)),
                pltpu.SemaphoreType.DMA((8,)),
            ],
            compiler_params=pltpu.CompilerParams(
                collective_id=0, has_side_effects=True, vmem_limit_bytes=24 * 2**20),
            name="convlstm",
        )(*(pltpu.with_memory_space_constraint(x, pltpu.HBM) for x in args))
        seq = jnp.concatenate([low, high], axis=1)
        return seq[:, None], c_last.reshape(c_init.shape)

    return jax.shard_map(local_run, mesh=mesh, in_specs=(seq_spec, P(), P(), P(), state_spec, state_spec),
                         out_specs=(seq_spec, state_spec), check_vma=False)
```

time: 95.2 us -> 92.2 us (0.968)
  Pallas kernels: 89.3 us -> 86.5 us
    pallas_call x1, Pallas kernels: 89.3 us -> 86.5 us  [local_run(): pl.pallas_call(functools.partial(kernel, steps, rows, cols, n_rows, n_col...]
where the time goes in v4:
time: 92.2 us; the launch traced here: 92.1 us
  Pallas kernels  86.5 us (94%)
  other arithmetic  4.02 us (4%)
    pallas_call x1, Pallas kernels, local_run(): pl.pallas_call(functools.partial(kernel, steps, rows, cols, n_rows, n_col...  86.5 us
    unnamed x1, other arithmetic  4.02 us

profile of v4, /device:TPU:0, one launch (start us, length us, event | category | flops | bytes accessed | tf_op | source)
XLA Modules:
  0.0 92.1 jit_solution(15649929662592713351)
XLA Ops:
  0.6 86.5 %convlstm.1 = (bf16[24,24,32,128]{3,2,1,0:T(8,128)(2,1)S(1)}, bf16[24,24,32,128]{3,2,1,0:T(8,128)(2,1)S(1)}, f32[1536,128]{1,0:T(8,128)S(1)}) custom-call(bf16[24,32,16,48]{3,2,1,0:T(8,128)(2,1)} %bitcast.14, bf16[1152,512]{1,0:T(8,128)(2,1)} %bitcast.15, bf16[144,512]{1,0:T(8,128)(2,1)} %bitcast.18, f32[1,512]{1,0:T(1,128)} %bitcast.19, ...), custom_call_target="tpu_custom_call" | custom-call | tf_op jit(solution)/shard_map/convlstm/pallas_call | solution.py:410
  87.2 4.0 %maximum_bitcast_fusion = bf16[24,1,48,32,128]{4,3,2,1,0:T(8,128)(2,1)} fusion(bf16[24,24,32,128]{3,2,1,0:T(8,128)(2,1)S(1)} %get-tuple-element.6, bf16[24,24,32,128]{3,2,1,0:T(8,128)(2,1)S(1)} %get-tuple-element.5), kind=kLoop, calls=%fused_computation | loop fusion | flops 4718592 | bytes 18874368
  91.2 0.9 copy.10

commit v5 on v4

--- a/solution.py
+++ b/solution.py
@@ -14,6 +14,7 @@
 
 PITCH = 36
 DIRECTIONS = ((-1, 0), (1, 0), (0, -1), (0, 1), (-1, -1), (-1, 1), (1, -1), (1, 1))
+CHUNK = 3
 BLOCK = 11
 SIDE = 4
 
@@ -27,10 +28,10 @@
 
 
 def kernel(steps, rows, cols, n_rows, n_cols, c_in, frames_ref, w_rec_ref, w_in_ref, bias_ref, h0_ref, c0_ref,
-           seq_low, seq_high, cout_ref,
+           seq_ref, cout_ref,
            x_buf, p_buf, w_buf, bias_buf, f_buf, f_side, c_main, c_col, c_row, ring_row, ring_col,
-           row_send, col_send, crow_send, ccol_send,
-           row_recv, col_recv, corner_recv, crow_recv, ccol_recv, ccorner_recv,
+           row_send, col_send, corner_send, crow_send, ccol_send,
+           row_recv, col_recv, corner_recv, crow_recv, ccol_recv,
            send_sem, recv_sem, f_sem, f_send_sem, f_recv_sem, arg_sem):
     my_row = lax.axis_index("rows")
     my_col = lax.axis_index("cols")
@@ -38,9 +39,9 @@
     gates_n = 4 * hid
     packed = 3 * c_in
     width = cols - 2 * SIDE
-    half = rows // 2
     long = rows + 8
     side_cols = tuple(range(SIDE)) + tuple(range(cols - SIDE, cols))
+    last = len(side_cols) - 1
     edge_rows = (0, 1, rows - 2, rows - 1)
 
     def exists(d):
@@ -62,10 +63,7 @@
     def source(slot, d, kind):
         dr, dc = DIRECTIONS[d]
         if dr and dc:
-            k = 0 if dc < 0 else 1
-            if kind:
-                return ccol_send.at[slot, k, pl.ds(0 if dr < 0 else rows - 8, 8)]
-            return col_send.at[slot, k, :, pl.ds(0 if dr < 0 else rows - 16, 16)]
+            return corner_send.at[slot, d - 4]
         if dr:
             return (crow_send if kind else row_send).at[slot, d]
         return (ccol_send if kind else col_send).at[slot, d - 2]
@@ -73,7 +71,7 @@
     def landing(slot, d, kind):
         dr, dc = DIRECTIONS[d]
         if dr and dc:
-            return (ccorner_recv if kind else corner_recv).at[slot, d - 4]
+            return corner_recv.at[slot, d - 4]
         if dr:
             return (crow_recv if kind else row_recv).at[slot, d]
         return (ccol_recv if kind else col_recv).at[slot, d - 2]
@@ -103,15 +101,14 @@
         ts = frame_part(part)
         return pltpu.make_async_copy(frames_ref.at[ts], f_buf.at[ts], f_sem.at[part])
 
-    loads = [(h0_ref.at[pl.ds(0, half)], seq_low.at[steps - 1]), (h0_ref.at[pl.ds(half, half)], seq_high.at[steps - 1]),
-             (c0_ref, cout_ref), (w_rec_ref, w_buf.at[pl.ds(0, 9 * hid)]), (bias_ref, bias_buf)]
+    loads = [(h0_ref, seq_ref.at[steps - 1]), (c0_ref, cout_ref), (w_rec_ref, w_buf.at[pl.ds(0, 9 * hid)]), (bias_ref, bias_buf)]
     loads += [(w_in_ref.at[pl.ds(packed * dy, packed)], w_buf.at[pl.ds(9 * hid + 128 * dy, packed)]) for dy in range(3)]
     loads = [pltpu.make_async_copy(src, dst, arg_sem.at[k]) for k, (src, dst) in enumerate(loads)]
     frame_load(0).start()
     for load in loads:
         load.start()
     frame_load(1).start()
-    for ref in (row_recv, col_recv, corner_recv, crow_recv, ccol_recv, ccorner_recv, f_side):
+    for ref in (row_recv, col_recv, corner_recv, crow_recv, ccol_recv, f_side):
         ref[...] = jnp.zeros_like(ref)
     for slot in range(2):
         x_buf[slot, pl.ds(0, 2 * PITCH), :] = jnp.zeros((2 * PITCH, hid), F32)
@@ -144,12 +141,10 @@
                 frame_side(part, d, True).wait_recv()
 
     send_sides(0)
-    for load in loads[:2]:
-        load.wait()
+    loads[0].wait()
     for r in range(rows):
-        part, at = (seq_low, r) if r < half else (seq_high, r - half)
-        x_buf[0, pl.ds(cell(r, 0), cols), :] = part[steps - 1, at].astype(F32)
-    loads[2].wait()
+        x_buf[0, pl.ds(cell(r, 0), cols), :] = seq_ref[steps - 1, r].astype(F32)
+    loads[1].wait()
     for r in range(2, rows - 2):
         c_main[pl.ds((r - 2) * width, width), :] = cout_ref[pl.ds(r * cols + SIDE, width), :]
     for i, c in enumerate(side_cols):
@@ -160,7 +155,7 @@
 
     lane = lax.broadcasted_iota(jnp.int32, (1, gates_n), 1)
     scale = jnp.where(lane < 3 * hid, 0.5, 1.0)
-    for load in loads[3:]:
+    for load in loads[2:]:
         load.wait()
     for at in range(0, 9 * hid, 128):
         w_buf[pl.ds(at, 128), :] = (w_buf[pl.ds(at, 128), :].astype(F32) * scale).astype(BF16)
@@ -242,21 +237,30 @@
         for k, c in enumerate((0, cols - 2)):
             for n in range(2):
                 col_send[slot, k, n] = state[pl.ds(cell(0, c + n), rows, stride=PITCH), :].astype(BF16)
-            ccol_send[slot, k] = c_col[pl.ds((0 if k == 0 else 2 * SIDE - 1) * rows, rows), :]
-
-    def send_halo(slot, wanted):
-        for d in range(8):
-            @pl.when(jnp.logical_and(exists(d), wanted))
-            def _():
-                departure(slot, d, 0).start()
-                departure(slot, d, 1).start()
+            ccol_send[slot, k] = c_col[pl.ds((0 if k == 0 else last) * rows, rows), :]
+        for k, (dr, dc) in enumerate(DIRECTIONS[4:]):
+            r, c = (0 if dr < 0 else rows - 2), (0 if dc < 0 else cols - 2)
+            for n in range(2):
+                corner = state[pl.ds(cell(r + n, c), 2), :].astype(BF16).astype(F32)
+                corner_send[slot, k, 2 * n:2 * n + 2] = corner
+            c_at = (0 if dr < 0 else 3 * cols) + (0 if dc < 0 else cols - 1)
+            corner_send[slot, k, 4:5] = c_row[pl.ds(c_at, 1), :]
+
+    def each_copy(act, slot, wanted=None):
+        for kind in range(2):
+            for d in range(8 if kind == 0 else 4):
+                @pl.when(exists(d) if wanted is None else jnp.logical_and(exists(d), wanted))
+                def _():
+                    act(slot, d, kind)
+
+    def send_halo(slot, wanted=None):
+        each_copy(lambda *which: departure(*which).start(), slot, wanted)
 
     def receive_halo(slot):
-        for d in range(8):
-            @pl.when(exists(d))
-            def _():
-                arrival(slot, d, 0).wait_recv()
-                arrival(slot, d, 1).wait_recv()
+        each_copy(lambda *which: arrival(*which).wait_recv(), slot)
+
+    def wait_sent(slot):
+        each_copy(lambda *which: departure(*which).wait_send(), slot)
 
     def unpack_halo(slot, p_first):
         state = x_buf.at[0]
@@ -274,25 +278,15 @@
                 state[pl.ds(cell(0, c + n), rows, stride=PITCH), :] = col_recv[slot, k, n].astype(F32)
             ring_col[pl.ds(k * long + 1, rows), :] = ccol_recv[slot, k]
         for k, (dr, dc) in enumerate(DIRECTIONS[4:]):
-            r, pick = (-2, 14) if dr < 0 else (rows, 0)
-            c = -2 if dc < 0 else cols
-            for n in range(2):
-                state[pl.ds(cell(r, c + n), 2, stride=PITCH), :] = corner_recv[slot, k, n].astype(F32)[pick:pick + 2]
+            r, c = (-2 if dr < 0 else rows), (-2 if dc < 0 else cols)
+            for n in range(2):
+                state[pl.ds(cell(r + n, c), 2), :] = corner_recv[slot, k, 2 * n:2 * n + 2]
             at = (0 if dc < 0 else long) + (0 if dr < 0 else rows + 1)
-            pick = 7 if dr < 0 else 0
-            ring_col[pl.ds(at, 1), :] = ccorner_recv[slot, k][pick:pick + 1]
-
-    def wait_sent(slot):
-        for d in range(8):
-            @pl.when(exists(d))
-            def _():
-                departure(slot, d, 0).wait_send()
-                departure(slot, d, 1).wait_send()
+            ring_col[pl.ds(at, 1), :] = corner_recv[slot, k, 4:5]
 
     def write_out(t, slot):
         for r in range(rows):
-            part, at = (seq_low, r) if r < half else (seq_high, r - half)
-            part[t, at] = x_buf[slot, pl.ds(cell(r, 0), cols), :].astype(BF16)
+            seq_ref[t, r] = x_buf[slot, pl.ds(cell(r, 0), cols), :].astype(BF16)
 
     def main_run(first, last):
         return [(r, SIDE, width, False) for r in range(first, last)]
@@ -313,7 +307,6 @@
     ring_row_run = [(-1, 0, cols, False), (rows, 0, cols, False)]
     row_run = [(r, 0, cols, False) for r in edge_rows]
     n_long = 2 * long
-    last = 2 * SIDE - 1
 
     def pair(m, now):
         t = 2 * m
@@ -367,7 +360,7 @@
     pack_frame(0, 0)
     pack_frame(1, 1)
     stage(0, 0)
-    send_halo(0, True)
+    send_halo(0)
     receive_sides(1)
 
     def trip(i, carry):
@@ -392,6 +385,16 @@
                 frame_side(part, d).wait_send()
 
 
+def write_back(seq_in, c_in, seq_out, c_out, sem):
+    copies = [pltpu.make_async_copy(seq_in.at[pl.ds(t, CHUNK)], seq_out.at[pl.ds(t, CHUNK)], sem.at[1 + t // CHUNK])
+              for t in range(0, seq_in.shape[0], CHUNK)]
+    copies.append(pltpu.make_async_copy(c_in, c_out, sem.at[0]))
+    for copy in copies:
+        copy.start()
+    for copy in copies:
+        copy.wait()
+
+
 def solution(mesh):
     n_rows = mesh.shape["rows"]
     n_cols = mesh.shape["cols"]
@@ -402,17 +405,18 @@
         steps, _, rows, cols, c_in = frames.shape
         hid = h_init.shape[-1]
         row_words = 2 * cols + 3 * PITCH + 4
+        both = (2, 2)
         vmem = pl.BlockSpec(memory_space=pltpu.VMEM)
         args = (jnp.transpose(frames[:, 0], (0, 2, 3, 1)), w_rec.reshape(9 * hid, 4 * hid),
                 w_in.reshape(9 * c_in, 4 * hid), gate_bias.reshape(1, 4 * hid), h_init[0],
                 c_init[0].reshape(rows * cols, hid))
         hbm = pl.BlockSpec(memory_space=pltpu.HBM)
-        low, high, c_last = pl.pallas_call(
+        seq, c_last = pl.pallas_call(
             functools.partial(kernel, steps, rows, cols, n_rows, n_cols, c_in),
-            out_shape=(jax.ShapeDtypeStruct((steps, rows // 2, cols, hid), BF16),) * 2 + (
-                jax.ShapeDtypeStruct((rows * cols, hid), F32),),
+            out_shape=(jax.ShapeDtypeStruct((steps, rows, cols, hid), BF16),
+                       jax.ShapeDtypeStruct((rows * cols, hid), F32)),
             in_specs=[hbm] * 6,
-            out_specs=(vmem,) * 3,
+            out_specs=(vmem, vmem),
             scratch_shapes=[
                 pltpu.VMEM((2, (rows + 12) * PITCH, hid), F32),
                 pltpu.VMEM((4, (rows + 12) * PITCH, 128), F32),
@@ -425,28 +429,36 @@
                 pltpu.VMEM((cols * 4, hid), F32),
                 pltpu.VMEM((cols * 2, hid), F32),
                 pltpu.VMEM(((rows + 8) * 2, hid), F32),
-                pltpu.VMEM((2, 2, row_words, hid), BF16),
-                pltpu.VMEM((2, 2, 2, rows, hid), BF16),
-                pltpu.VMEM((2, 2, cols, hid), F32),
-                pltpu.VMEM((2, 2, rows, hid), F32),
-                pltpu.VMEM((2, 2, row_words, hid), BF16),
-                pltpu.VMEM((2, 2, 2, rows, hid), BF16),
-                pltpu.VMEM((2, 4, 2, 16, hid), BF16),
-                pltpu.VMEM((2, 2, cols, hid), F32),
-                pltpu.VMEM((2, 2, rows, hid), F32),
+                pltpu.VMEM((*both, row_words, hid), BF16),
+                pltpu.VMEM((*both, 2, rows, hid), BF16),
                 pltpu.VMEM((2, 4, 8, hid), F32),
-                pltpu.SemaphoreType.DMA((2, 2, 8)),
-                pltpu.SemaphoreType.DMA((2, 2, 8)),
+                pltpu.VMEM((*both, cols, hid), F32),
+                pltpu.VMEM((*both, rows, hid), F32),
+                pltpu.VMEM((*both, row_words, hid), BF16),
+                pltpu.VMEM((*both, 2, rows, hid), BF16),
+                pltpu.VMEM((2, 4, 8, hid), F32),
+                pltpu.VMEM((*both, cols, hid), F32),
+                pltpu.VMEM((*both, rows, hid), F32),
+                pltpu.SemaphoreType.DMA((*both, 8)),
+                pltpu.SemaphoreType.DMA((*both, 8)),
                 pltpu.SemaphoreType.DMA((2,)),
-                pltpu.SemaphoreType.DMA((2, 2)),
-                pltpu.SemaphoreType.DMA((2, 2)),
-                pltpu.SemaphoreType.DMA((8,)),
+                pltpu.SemaphoreType.DMA(both),
+                pltpu.SemaphoreType.DMA(both),
+                pltpu.SemaphoreType.DMA((7,)),
             ],
             compiler_params=pltpu.CompilerParams(
                 collective_id=0, has_side_effects=True, vmem_limit_bytes=24 * 2**20),
             name="convlstm",
         )(*(pltpu.with_memory_space_constraint(x, pltpu.HBM) for x in args))
-        seq = jnp.concatenate([low, high], axis=1)
+        seq, c_last = pl.pallas_call(
+            write_back,
+            out_shape=(jax.ShapeDtypeStruct(seq.shape, BF16), jax.ShapeDtypeStruct(c_last.shape, F32)),
+            in_specs=[vmem] * 2,
+            out_specs=(hbm, hbm),
+            scratch_shapes=[pltpu.SemaphoreType.DMA((2 + steps // CHUNK,))],
+            compiler_params=pltpu.CompilerParams(vmem_limit_bytes=2**20),
+            name="write_back",
+        )(seq, c_last)
         return seq[:, None], c_last.reshape(c_init.shape)
 
     return jax.shard_map(local_run, mesh=mesh, in_specs=(seq_spec, P(), P(), P(), state_spec, state_spec),

time: 92.2 us -> 88.5 us (0.960)
  other arithmetic: 4.02 us -> 0 us
  Pallas kernels: 86.5 us -> 87.7 us
    unnamed x1 -> x0, other arithmetic: 4.02 us -> none
    pallas_call x0 -> x1, Pallas kernels: none -> 3.94 us  [local_run(): pl.pallas_call(write_back, out_shape=(jax.ShapeDtypeStruct(seq.shape, BF1...]
    pallas_call x1, Pallas kernels: 86.5 us -> 83.7 us  [local_run(): pl.pallas_call(functools.partial(kernel, steps, rows, cols, n_rows, n_col...]
where the time goes in v5:
time: 88.5 us; the launch traced here: 88.3 us
  Pallas kernels  87.7 us (99%)
    pallas_call x1, Pallas kernels, local_run(): pl.pallas_call(functools.partial(kernel, steps, rows, cols, n_rows, n_col...  83.7 us
    pallas_call x1, Pallas kernels, local_run(): pl.pallas_call(write_back, out_shape=(jax.ShapeDtypeStruct(seq.shape, BF1...  3.94 us

profile of v5, /device:TPU:0, one launch (start us, length us, event | category | flops | bytes accessed | tf_op | source)
XLA Modules:
  0.0 88.3 jit_solution(6511927892102008341)
XLA Ops:
  0.6 83.7 %convlstm.1 = (bf16[24,48,32,128]{3,2,1,0:T(8,128)(2,1)S(1)}, f32[1536,128]{1,0:T(8,128)S(1)}) custom-call(bf16[24,32,16,48]{3,2,1,0:T(8,128)(2,1)} %bitcast.12, bf16[1152,512]{1,0:T(8,128)(2,1)} %bitcast.13, bf16[144,512]{1,0:T(8,128)(2,1)} %bitcast.16, f32[1,512]{1,0:T(1,128)} %bitcast.17, bf16[48,32,128]{2,1,0:T(8,128)(2,1)} %bitcast.15, f32[1536,128]{1,0:T(8,128)} %bitcast.14), custom_call_target="tpu_custom_call" | custom-call | tf_op jit(solution)/shard_map/convlstm/pallas_call | solution.py:414
  84.4 3.9 %write_back.1 = (bf16[24,48,32,128]{3,2,1,0:T(8,128)(2,1)}, f32[1536,128]{1,0:T(8,128)}) custom-call(bf16[24,48,32,128]{3,2,1,0:T(8,128)(2,1)S(1)} %get-tuple-element.6.seq_in, f32[1536,128]{1,0:T(8,128)S(1)} %get-tuple-element.7.c_in), custom_call_target="tpu_custom_call" | custom-call | tf_op jit(solution)/shard_map/write_back/pallas_call | solution.py:453

commit v6 on v5

v6 whole, which is shorter than its diff:
```python
import functools

import jax
import jax.numpy as jnp
from jax import lax
from jax.experimental import pallas as pl
from jax.experimental.pallas import tpu as pltpu
from jax.sharding import PartitionSpec as P

MESH = pl.DeviceIdType.MESH
LANES = 128
BF16 = jnp.bfloat16
F32 = jnp.float32
TDT = jnp.bfloat16

PITCH = 36
DIRECTIONS = ((-1, 0), (1, 0), (0, -1), (0, 1), (-1, -1), (-1, 1), (1, -1), (1, 1))
CHUNK = 2
FIRST, STOP = 13, 29
BLOCK = 11
SIDE = 4


def cell(r, c):
    return (r + 2) * PITCH + c + 2


def pcell(r, c):
    return (r + 2) * PITCH + c + 1


def exists(d, n_rows, n_cols):
    dr, dc = DIRECTIONS[d]
    ok = None
    for here, step, count in ((lax.axis_index("rows"), dr, n_rows), (lax.axis_index("cols"), dc, n_cols)):
        if step:
            this = (here > 0) if step < 0 else (here < count - 1)
            ok = this if ok is None else jnp.logical_and(ok, this)
    return ok


class Tile:
    def __init__(self, sizes, x_buf, p_buf, w_buf, c_main, c_col, c_row, ring_row, ring_col):
        self.steps, self.rows, self.cols, self.n_rows, self.n_cols, self.c_in = sizes
        self.x_buf, self.p_buf, self.w_buf = x_buf, p_buf, w_buf
        self.c_main, self.c_col, self.c_row = c_main, c_col, c_row
        self.ring_row, self.ring_col = ring_row, ring_col
        self.hid = x_buf.shape[-1]
        self.width = self.cols - 2 * SIDE
        self.long = self.rows + 8
        self.side_cols = tuple(range(SIDE)) + tuple(range(self.cols - SIDE, self.cols))
        self.edge_rows = (0, 1, self.rows - 2, self.rows - 1)
        self.last = len(self.side_cols) - 1

    def run_index(self, start, length, vertical):
        return pl.ds(start, length, stride=PITCH) if vertical else pl.ds(start, length)

    def gates_of(self, slot, p_slot, groups):
        parts = []
        for dy in range(3):
            for dx in range(3):
                pieces = [self.x_buf[slot, self.run_index(cell(r + dy - 1, c + dx - 1), length, vertical), :]
                          for r, c, length, vertical in groups]
                parts.append(jnp.concatenate(pieces, axis=0) if len(pieces) > 1 else pieces[0])
        for dy in range(3):
            pieces = [self.p_buf[p_slot, self.run_index(pcell(r + dy - 1, c), length, vertical), :]
                      for r, c, length, vertical in groups]
            parts.append(jnp.concatenate(pieces, axis=0) if len(pieces) > 1 else pieces[0])
        lhs = jnp.concatenate(parts, axis=1).astype(BF16)
        return jnp.dot(lhs, self.w_buf[...], preferred_element_type=F32)

    def finish(self, slot, groups, gates, c_ref, c_at, mask=None):
        index = pl.ds(c_at, gates.shape[0])
        c_prev = c_ref[index, :]
        gi, gf, go, gg = (jnp.tanh(gates[:, self.hid * k:self.hid * (k + 1)]) for k in range(4))
        c_next = 0.5 * ((gf * c_prev + c_prev) + (gi * gg + gg))
        h = (0.5 * go + 0.5) * jnp.tanh(c_next)
        if mask is None:
            c_ref[index, :] = c_next
        else:
            h = h * mask
        at = 0
        for r, c, length, vertical in groups:
            self.x_buf[1 - slot, self.run_index(cell(r, c), length, vertical), :] = h[at:at + length]
            at += length

    def update(self, slot, p_slot, groups, c_ref, c_at):
        self.finish(slot, groups, self.gates_of(slot, p_slot, groups), c_ref, c_at)

    def main_run(self, first, stop):
        return [(r, SIDE, self.width, False) for r in range(first, stop)]

    def side_run(self, *ids):
        return [(0, self.side_cols[i], self.rows, True) for i in ids]

    def main_rows(self, slot, p_slot, first, stop):
        self.update(slot, p_slot, self.main_run(first, stop), self.c_main, (first - 2) * self.width)

    def write_out(self, slot, ref):
        for r in range(self.rows):
            ref[r] = self.x_buf[slot, pl.ds(cell(r, 0), self.cols), :].astype(BF16)

    def before_wait(self, pa, write):
        rows, last = self.rows, self.last
        for at in range(2, rows - 2, BLOCK):
            self.main_rows(0, pa, at, at + BLOCK)
        self.update(0, pa, self.side_run(1, 2, 3), self.c_col, rows)
        self.update(0, pa, self.side_run(last - 3, last - 2, last - 1), self.c_col, (last - 3) * rows)
        write()
        for first, stop in ((3, FIRST), (STOP, rows - 11), (rows - 11, rows - 3)):
            self.main_rows(1, pa + 1, first, stop)

    def after_wait(self, pa, send):
        rows, cols, last = self.rows, self.cols, self.last
        there = [jnp.where(exists(d, self.n_rows, self.n_cols), 1.0, 0.0).astype(F32) for d in range(4)]
        place = lax.broadcasted_iota(jnp.int32, (self.long, self.hid), 0)
        ends = jnp.where(place == 0, there[0], jnp.where(place == rows + 1, there[1], 1.0))
        ring_col_run = [(-1, -1, self.long, True), (-1, cols, self.long, True)]
        ring_row_run = [(-1, 0, cols, False), (rows, 0, cols, False)]
        row_run = [(r, 0, cols, False) for r in self.edge_rows]
        n_long = 2 * self.long
        middle = (FIRST + STOP) // 2
        c_col, c_row, c_main, finish = self.c_col, self.c_row, self.c_main, self.finish

        own = self.side_run(0) + self.side_run(last) + row_run
        own_gates = self.gates_of(0, pa, own)
        ring_gates = self.gates_of(0, pa, ring_col_run + ring_row_run)
        run = self.main_run(FIRST, middle)
        beside = self.gates_of(1, pa + 1, run)
        finish(0, self.side_run(0), own_gates[:rows], c_col, 0)
        finish(0, self.side_run(last), own_gates[rows:2 * rows], c_col, last * rows)
        finish(0, row_run, own_gates[2 * rows:], c_row, 0)
        mask = jnp.concatenate([ends * there[2], ends * there[3]], axis=0)
        finish(0, ring_col_run, ring_gates[:n_long], self.ring_col, 0, mask)
        mask = jnp.concatenate([jnp.full((cols, self.hid), 1.0, F32) * there[k] for k in range(2)], axis=0)
        finish(0, ring_row_run, ring_gates[n_long:], self.ring_row, 0, mask)
        for i, r in ((0, 0), (3, rows - 1)):
            for first in (1, last - 3):
                c_col[pl.ds(first * rows + r, 3, stride=rows), :] = c_row[pl.ds(i * cols + self.side_cols[first], 3), :]
        finish(1, run, beside, c_main, (FIRST - 2) * self.width)
        edge_gates = self.gates_of(1, pa + 1, self.side_run(0, 1, last - 1, last) + row_run)
        run = self.main_run(middle, STOP)
        beside = self.gates_of(1, pa + 1, run)
        finish(1, self.side_run(0, 1), edge_gates[:2 * rows], c_col, 0)
        finish(1, self.side_run(last - 1, last), edge_gates[2 * rows:4 * rows], c_col, (last - 1) * rows)
        finish(1, row_run, edge_gates[4 * rows:], c_row, 0)
        send()

        finish(1, run, beside, c_main, (middle - 2) * self.width)
        runs = [(self.side_run(2, 3), c_col, 2 * rows), (self.side_run(last - 3, last - 2), c_col, (last - 3) * rows),
                (self.main_run(2, 3), c_main, 0), (self.main_run(rows - 3, rows - 2), c_main, (rows - 5) * self.width)]
        gates = self.gates_of(1, pa + 1, sum((run for run, _, _ in runs), []))
        at = 0
        for run, c_ref, c_at in runs:
            size = sum(length for _, _, length, _ in run)
            finish(1, run, gates[at:at + size], c_ref, c_at)
            at += size


def kernel(sizes, frames_ref, w_rec_ref, w_in_ref, bias_ref, h0_ref, c0_ref,
           seq_ref, x_buf, p_buf, w_buf, c_main, c_col, c_row, ring_row, ring_col,
           bias_buf, f_buf, f_side, c_buf, row_send, col_send, corner_send, crow_send, ccol_send,
           row_recv, col_recv, corner_recv, crow_recv, ccol_recv,
           send_sem, recv_sem, f_sem, f_send_sem, f_recv_sem, arg_sem):
    tile = Tile(sizes, x_buf, p_buf, w_buf, c_main, c_col, c_row, ring_row, ring_col)
    steps, rows, cols, n_rows, n_cols, c_in = sizes
    hid, width, long, last = tile.hid, tile.width, tile.long, tile.last
    side_cols, edge_rows = tile.side_cols, tile.edge_rows
    gates_n = 4 * hid
    packed = 3 * c_in
    my_row = lax.axis_index("rows")
    my_col = lax.axis_index("cols")

    def device(d):
        dr, dc = DIRECTIONS[d]
        return {"rows": my_row + dr, "cols": my_col + dc}

    def opposite(d):
        return DIRECTIONS.index((-DIRECTIONS[d][0], -DIRECTIONS[d][1]))

    def source(slot, d, kind):
        dr, dc = DIRECTIONS[d]
        if dr and dc:
            return corner_send.at[slot, d - 4]
        if dr:
            return (crow_send if kind else row_send).at[slot, d]
        return (ccol_send if kind else col_send).at[slot, d - 2]

    def landing(slot, d, kind):
        dr, dc = DIRECTIONS[d]
        if dr and dc:
            return corner_recv.at[slot, d - 4]
        if dr:
            return (crow_recv if kind else row_recv).at[slot, d]
        return (ccol_recv if kind else col_recv).at[slot, d - 2]

    def departure(slot, d, kind):
        return pltpu.make_async_remote_copy(
            src_ref=source(slot, d, kind), dst_ref=landing(slot, opposite(d), kind), send_sem=send_sem.at[slot, kind, d],
            recv_sem=recv_sem.at[slot, kind, opposite(d)], device_id=device(d), device_id_type=MESH)

    def arrival(slot, d, kind):
        return pltpu.make_async_remote_copy(
            src_ref=source(slot, d, kind), dst_ref=landing(slot, d, kind), send_sem=send_sem.at[slot, kind, d],
            recv_sem=recv_sem.at[slot, kind, d], device_id=device(d), device_id_type=MESH)

    def frame_part(part):
        return pl.ds(0, 2) if part == 0 else pl.ds(2, steps - 2)

    def frame_side(part, d, arriving=False):
        ts = frame_part(part)
        k = d - 2
        at = k if arriving else 1 - k
        return pltpu.make_async_remote_copy(
            src_ref=f_buf.at[ts, pl.ds(0 if k == 0 else cols - 2, 2)], dst_ref=f_side.at[at, ts],
            send_sem=f_send_sem.at[part, k], recv_sem=f_recv_sem.at[part, at], device_id=device(d), device_id_type=MESH)

    def frame_load(part):
        ts = frame_part(part)
        return pltpu.make_async_copy(frames_ref.at[ts], f_buf.at[ts], f_sem.at[part])

    loads = [(h0_ref, seq_ref.at[steps - 1]), (c0_ref, c_buf), (w_rec_ref, w_buf.at[pl.ds(0, 9 * hid)]), (bias_ref, bias_buf)]
    loads += [(w_in_ref.at[pl.ds(packed * dy, packed)], w_buf.at[pl.ds(9 * hid + LANES * dy, packed)]) for dy in range(3)]
    loads = [pltpu.make_async_copy(src, dst, arg_sem.at[k]) for k, (src, dst) in enumerate(loads)]
    frame_load(0).start()
    for load in loads:
        load.start()
    frame_load(1).start()
    for ref in (row_recv, col_recv, corner_recv, crow_recv, ccol_recv, f_side):
        ref[...] = jnp.zeros_like(ref)
    for slot in range(2):
        x_buf[slot, pl.ds(0, 2 * PITCH), :] = jnp.zeros((2 * PITCH, hid), F32)
        x_buf[slot, pl.ds((rows + 2) * PITCH, 10 * PITCH), :] = jnp.zeros((10 * PITCH, hid), F32)
    for slot in range(4):
        p_buf[slot, pl.ds(0, 2 * PITCH), :] = jnp.zeros((2 * PITCH, LANES), F32)
        p_buf[slot, pl.ds((rows + 2) * PITCH, 10 * PITCH), :] = jnp.zeros((10 * PITCH, LANES), F32)
    ring_col[...] = jnp.zeros_like(ring_col)

    barrier = pltpu.get_barrier_semaphore()
    count = jnp.int32(0)
    for d in range(8):
        @pl.when(exists(d, n_rows, n_cols))
        def _():
            pl.semaphore_signal(barrier, inc=1, device_id=device(d), device_id_type=MESH)
        count = count + exists(d, n_rows, n_cols).astype(jnp.int32)
    pl.semaphore_wait(barrier, count)

    def send_sides(part):
        frame_load(part).wait()
        for d in (2, 3):
            @pl.when(exists(d, n_rows, n_cols))
            def _():
                frame_side(part, d).start()

    def receive_sides(part):
        for d in (2, 3):
            @pl.when(exists(d, n_rows, n_cols))
            def _():
                frame_side(part, d, True).wait_recv()

    send_sides(0)
    loads[0].wait()
    for r in range(rows):
        x_buf[0, pl.ds(cell(r, 0), cols), :] = seq_ref[steps - 1, r].astype(F32)
    loads[1].wait()
    for r in range(2, rows - 2):
        c_main[pl.ds((r - 2) * width, width), :] = c_buf[pl.ds(r * cols + SIDE, width), :]
    for i, c in enumerate(side_cols):
        c_col[pl.ds(i * rows, rows), :] = c_buf[pl.ds(c, rows, stride=cols), :]
    for i, r in enumerate(edge_rows):
        c_row[pl.ds(i * cols, cols), :] = c_buf[pl.ds(r * cols, cols), :]
    send_sides(1)

    lane = lax.broadcasted_iota(jnp.int32, (1, gates_n), 1)
    scale = jnp.where(lane < 3 * hid, 0.5, 1.0)
    for load in loads[2:]:
        load.wait()
    for at in range(0, 9 * hid, LANES):
        w_buf[pl.ds(at, LANES), :] = (w_buf[pl.ds(at, LANES), :].astype(F32) * scale).astype(BF16)
    bias = bias_buf[...] * scale
    b0 = bias.astype(BF16).astype(F32)
    b1 = (bias - b0).astype(BF16).astype(F32)
    b2 = bias - b0 - b1
    row = lax.broadcasted_iota(jnp.int32, (16, gates_n), 0)
    bias_rows = jnp.where(row == 0, b0, jnp.where(row == 1, b1, jnp.where(row == 2, b2, 0.0)))
    for dy in range(3):
        at = 9 * hid + LANES * dy
        w_buf[pl.ds(at, packed), :] = (w_buf[pl.ds(at, packed), :].astype(F32) * scale).astype(BF16)
        w_buf[pl.ds(at + packed, LANES - packed), :] = jnp.zeros((LANES - packed, gates_n), BF16)
        if dy == 1:
            w_buf[pl.ds(at + packed, 16), :] = bias_rows.astype(BF16)

    row = lax.broadcasted_iota(jnp.int32, (LANES - packed, rows), 0)
    ones = jnp.where(row < 3, 1.0, 0.0).astype(BF16)

    def pack_frame(t, slot):
        for c in range(-1, cols + 1):
            pieces = []
            for k in range(c - 1, c + 2):
                if k < 0:
                    pieces.append(f_side[0, t, k + 2])
                elif k < cols:
                    pieces.append(f_buf[t, k])
                else:
                    pieces.append(f_side[1, t, k - cols])
            window = jnp.concatenate(pieces + [ones], axis=0)
            p_buf[slot, pl.ds(pcell(0, c), rows, stride=PITCH), :] = window.T.astype(F32)

    def stage(slot, p_first):
        state = x_buf.at[0]
        for k, r in enumerate((0, rows - 2)):
            for n in range(2):
                row_send[slot, k, n * cols:(n + 1) * cols] = state[pl.ds(cell(r + n, 0), cols), :].astype(BF16)
            at = 2 * cols
            row_send[slot, k, at:at + 2 * PITCH] = p_buf[p_first, pl.ds(pcell(r, -1), 2 * PITCH), :].astype(BF16)
            at += 2 * PITCH
            r_one = 0 if k == 0 else rows - 1
            row_send[slot, k, at:at + PITCH] = p_buf[p_first + 1, pl.ds(pcell(r_one, -1), PITCH), :].astype(BF16)
            crow_send[slot, k] = c_row[pl.ds((0 if k == 0 else 3) * cols, cols), :]
        for k, c in enumerate((0, cols - 2)):
            for n in range(2):
                col_send[slot, k, n] = state[pl.ds(cell(0, c + n), rows, stride=PITCH), :].astype(BF16)
            ccol_send[slot, k] = c_col[pl.ds((0 if k == 0 else last) * rows, rows), :]
        for k, (dr, dc) in enumerate(DIRECTIONS[4:]):
            r, c = (0 if dr < 0 else rows - 2), (0 if dc < 0 else cols - 2)
            for n in range(2):
                corner = state[pl.ds(cell(r + n, c), 2), :].astype(BF16).astype(F32)
                corner_send[slot, k, 2 * n:2 * n + 2] = corner
            c_at = (0 if dr < 0 else 3 * cols) + (0 if dc < 0 else cols - 1)
            corner_send[slot, k, 4:5] = c_row[pl.ds(c_at, 1), :]

    def each_copy(act, slot, wanted=None):
        for kind in range(2):
            for d in range(8 if kind == 0 else 4):
                @pl.when(exists(d, n_rows, n_cols) if wanted is None else jnp.logical_and(exists(d, n_rows, n_cols), wanted))
                def _():
                    act(slot, d, kind)

    def send_halo(slot, wanted=None):
        each_copy(lambda *which: departure(*which).start(), slot, wanted)

    def receive_halo(slot):
        each_copy(lambda *which: arrival(*which).wait_recv(), slot)

    def wait_sent(slot):
        each_copy(lambda *which: departure(*which).wait_send(), slot)

    def unpack_halo(slot, p_first):
        state = x_buf.at[0]
        for k, r in enumerate((-2, rows)):
            for n in range(2):
                state[pl.ds(cell(r + n, 0), cols), :] = row_recv[slot, k, n * cols:(n + 1) * cols].astype(F32)
            at = 2 * cols
            p_buf[p_first, pl.ds(pcell(r, -1), 2 * PITCH), :] = row_recv[slot, k, at:at + 2 * PITCH].astype(F32)
            at += 2 * PITCH
            r_one = -1 if k == 0 else rows
            p_buf[p_first + 1, pl.ds(pcell(r_one, -1), PITCH), :] = row_recv[slot, k, at:at + PITCH].astype(F32)
            ring_row[pl.ds(k * cols, cols), :] = crow_recv[slot, k]
        for k, c in enumerate((-2, cols)):
            for n in range(2):
                state[pl.ds(cell(0, c + n), rows, stride=PITCH), :] = col_recv[slot, k, n].astype(F32)
            ring_col[pl.ds(k * long + 1, rows), :] = ccol_recv[slot, k]
        for k, (dr, dc) in enumerate(DIRECTIONS[4:]):
            r, c = (-2 if dr < 0 else rows), (-2 if dc < 0 else cols)
            for n in range(2):
                state[pl.ds(cell(r + n, c), 2), :] = corner_recv[slot, k, 2 * n:2 * n + 2]
            at = (0 if dc < 0 else long) + (0 if dr < 0 else rows + 1)
            ring_col[pl.ds(at, 1), :] = corner_recv[slot, k, 4:5]

    receive_sides(0)
    pack_frame(0, 0)
    pack_frame(1, 1)
    stage(0, 0)
    send_halo(0)
    receive_sides(1)

    def before(m, now):
        t = 2 * m
        other = 2 * (1 - now)
        pack_frame(jnp.minimum(t + 2, steps - 2), other)
        pack_frame(jnp.minimum(t + 3, steps - 1), other + 1)
        tile.before_wait(2 * now, lambda: tile.write_out(0, seq_ref.at[jnp.maximum(t - 1, 0)]))

        @pl.when(m >= 1)
        def _():
            wait_sent(1 - now)
        receive_halo(now)
        unpack_halo(now, 2 * now)

    def pair(m, now):
        def send():
            stage(1 - now, 2 * (1 - now))
            send_halo(1 - now)

        before(m, now)
        tile.after_wait(2 * now, send)
        tile.write_out(1, seq_ref.at[2 * m])

    def trip(i, carry):
        pair(2 * i, 0)
        pair(2 * i + 1, 1)
        return carry

    n_pairs = steps // 2
    lax.fori_loop(0, (n_pairs - 1) // 2, trip, 0)
    for m in range(n_pairs - 2 + n_pairs % 2, n_pairs - 1):
        pair(m, m % 2)
    before(n_pairs - 1, (n_pairs - 1) % 2)
    wait_sent((n_pairs - 1) % 2)
    for part in (0, 1):
        for d in (2, 3):
            @pl.when(exists(d, n_rows, n_cols))
            def _():
                frame_side(part, d).wait_send()


def finish_kernel(sizes, seq_in, x_in, p_buf, w_buf, c_main_in, c_col_in, c_row_in, ring_row, ring_col,
                  seq_out, c_out, x_buf, c_main, c_col, c_row, out_buf, c_buf, sem):
    tile = Tile(sizes, x_buf, p_buf, w_buf, c_main, c_col, c_row, ring_row, ring_col)
    steps, rows, cols = sizes[:3]
    copies = [pltpu.make_async_copy(seq_in.at[pl.ds(t, CHUNK)], seq_out.at[pl.ds(t, CHUNK)], sem.at[t // CHUNK])
              for t in range(0, steps - 2, CHUNK)]
    for copy in copies:
        copy.start()
    tile.after_wait(2 * ((steps // 2 - 1) % 2), lambda: None)
    for slot in range(2):
        tile.write_out(1 - slot, out_buf.at[slot])
    for r in range(2, rows - 2):
        c_buf[pl.ds(r * cols + SIDE, tile.width), :] = c_main[pl.ds((r - 2) * tile.width, tile.width), :]
    for i, c in enumerate(tile.side_cols):
        c_buf[pl.ds(c, rows, stride=cols), :] = c_col[pl.ds(i * rows, rows), :]
    for i, r in enumerate(tile.edge_rows):
        c_buf[pl.ds(r * cols, cols), :] = c_row[pl.ds(i * cols, cols), :]
    tail = [pltpu.make_async_copy(out_buf, seq_out.at[pl.ds(steps - 2, 2)], sem.at[steps // CHUNK]),
            pltpu.make_async_copy(c_buf, c_out, sem.at[steps // CHUNK + 1])]
    for copy in tail:
        copy.start()
    for copy in copies + tail:
        copy.wait()


def solution(mesh):
    n_rows = mesh.shape["rows"]
    n_cols = mesh.shape["cols"]
    seq_spec = P(None, "dp", "rows", "cols", None)
    state_spec = P("dp", "rows", "cols", None)

    def local_run(frames, w_in, w_rec, gate_bias, h_init, c_init):
        steps, _, rows, cols, c_in = frames.shape
        hid = h_init.shape[-1]
        row_words = 2 * cols + 3 * PITCH + 4
        both = (2, 2)
        vmem = pl.BlockSpec(memory_space=pltpu.VMEM)
        args = (jnp.transpose(frames[:, 0], (0, 2, 3, 1)), w_rec.reshape(9 * hid, 4 * hid),
                w_in.reshape(9 * c_in, 4 * hid), gate_bias.reshape(1, 4 * hid), h_init[0],
                c_init[0].reshape(rows * cols, hid))
        hbm = pl.BlockSpec(memory_space=pltpu.HBM)
        sizes = (steps, rows, cols, n_rows, n_cols, c_in)

        def wide(*shape):
            return jax.ShapeDtypeStruct((*shape, hid), F32)

        state = (wide(2, (rows + 12) * PITCH), wide(4, (rows + 12) * PITCH),
                 jax.ShapeDtypeStruct((9 * hid + 3 * hid, 4 * hid), BF16), wide((rows - 4) * (cols - 2 * SIDE)),
                 wide(rows * 2 * SIDE), wide(cols * 4), wide(cols * 2), wide((rows + 8) * 2))
        seq_shape = jax.ShapeDtypeStruct((steps, rows, cols, hid), BF16)
        seq, *held = pl.pallas_call(
            functools.partial(kernel, sizes),
            out_shape=(seq_shape, *state),
            in_specs=[hbm] * 6,
            out_specs=(vmem,) * 9,
            scratch_shapes=[
                pltpu.VMEM((1, 4 * hid), F32),
                pltpu.VMEM((steps, cols, c_in, rows), BF16),
                pltpu.VMEM((2, steps, 2, c_in, rows), BF16),
                pltpu.VMEM((rows * cols, hid), F32),
                *[shape for _ in both for shape in (
                    pltpu.VMEM((*both, row_words, hid), BF16),
                    pltpu.VMEM((*both, 2, rows, hid), BF16),
                    pltpu.VMEM((2, 4, 8, hid), F32),
                    pltpu.VMEM((*both, cols, hid), F32),
                    pltpu.VMEM((*both, rows, hid), F32))],
                pltpu.SemaphoreType.DMA((*both, 8)),
                pltpu.SemaphoreType.DMA((*both, 8)),
                pltpu.SemaphoreType.DMA((2,)),
                pltpu.SemaphoreType.DMA(both),
                pltpu.SemaphoreType.DMA(both),
                pltpu.SemaphoreType.DMA((7,)),
            ],
            compiler_params=pltpu.CompilerParams(
                collective_id=0, has_side_effects=True, vmem_limit_bytes=14 * 2**20),
            name="convlstm",
        )(*(pltpu.with_memory_space_constraint(x, pltpu.HBM) for x in args))
        changed = (0, 3, 4, 5)
        seq, c_last, *_ = pl.pallas_call(
            functools.partial(finish_kernel, sizes),
            out_shape=(seq_shape, wide(rows * cols), *(state[k] for k in changed)),
            in_specs=[vmem] * 9,
            out_specs=(hbm, hbm, *[vmem] * len(changed)),
            input_output_aliases={1 + k: 2 + n for n, k in enumerate(changed)},
            scratch_shapes=[
                pltpu.VMEM((2, rows, cols, hid), BF16),
                pltpu.VMEM((rows * cols, hid), F32),
                pltpu.SemaphoreType.DMA((steps // CHUNK + 2,)),
            ],
            compiler_params=pltpu.CompilerParams(vmem_limit_bytes=6 * 2**20),
            name="finish",
        )(seq, *held)
        return seq[:, None], c_last.reshape(c_init.shape)

    return jax.shard_map(local_run, mesh=mesh, in_specs=(seq_spec, P(), P(), P(), state_spec, state_spec),
                         out_specs=(seq_spec, state_spec), check_vma=False)
```

time: 88.5 us -> 86.8 us (0.981)
  Pallas kernels: 87.7 us -> 85.9 us
    pallas_call x2, Pallas kernels: 87.7 us -> 85.9 us  [the longest x1 80.4 us: local_run(): pl.pallas_call(functools.partial(kernel, sizes), out_shape=(seq_shape, *s...]
where the time goes in v6:
time: 86.8 us; the launch traced here: 86.7 us
  Pallas kernels  85.9 us (99%)
    pallas_call x1, Pallas kernels, local_run(): pl.pallas_call(functools.partial(kernel, sizes), out_shape=(seq_shape, *s...  80.4 us
    pallas_call x1, Pallas kernels, local_run(): pl.pallas_call(functools.partial(finish_kernel, sizes), out_shape=(seq_sh...  5.51 us

profile of v6, /device:TPU:0, one launch (start us, length us, event | category | flops | bytes accessed | tf_op | source)
XLA Modules:
  0.0 86.7 jit_solution(14719064016159795122)
XLA Ops:
  0.6 80.4 %convlstm.1 = (bf16[24,48,32,128]{3,2,1,0:T(8,128)(2,1)S(1)}, f32[2,2160,128]{2,1,0:T(8,128)S(1)}, f32[4,2160,128]{2,1,0:T(8,128)S(1)}, bf16[1536,512]{1,0:T(8,1...) custom-call(bf16[24,32,16,48]{3,2,1,0:T(8,128)(2,1)} %bitcast.12, ...), custom_call_target="tpu_custom_call" | custom-call | tf_op jit(solution)/shard_map/convlstm/pallas_call | solution.py:467
  81.0 5.5 %finish.1 = (bf16[24,48,32,128]{3,2,1,0:T(8,128)(2,1)}, f32[1536,128]{1,0:T(8,128)}, f32[2,2160,128]{2,1,0:T(8,128)S(1)}, f32[1056,128]{1,0:T(8,128)S(1)}, f32[3...) custom-call(bf16[24,48,32,128]{3,2,1,0:T(8,128)(2,1)S(1)} %get-tuple, ...), custom_call_target="tpu_custom_call", output_to_operand_aliasing={{2}: (1, {}), {3}: (4, {}), {4}: (5, {}), {5}: (6, {})} | custom-call | tf_op jit(solution)/shard_map/finish/pallas_call | solution.py:495

commit v7 on v6

--- a/solution.py
+++ b/solution.py
@@ -16,6 +16,7 @@
 PITCH = 36
 DIRECTIONS = ((-1, 0), (1, 0), (0, -1), (0, 1), (-1, -1), (-1, 1), (1, -1), (1, 1))
 CHUNK = 2
+PARTS = (4, 12)
 FIRST, STOP = 13, 29
 BLOCK = 11
 SIDE = 4
@@ -112,7 +113,7 @@
 
     def after_wait(self, pa, send):
         rows, cols, last = self.rows, self.cols, self.last
-        there = [jnp.where(exists(d, self.n_rows, self.n_cols), 1.0, 0.0).astype(F32) for d in range(4)]
+        there = [exists(d, self.n_rows, self.n_cols).astype(jnp.int32).astype(F32) for d in range(4)]
         place = lax.broadcasted_iota(jnp.int32, (self.long, self.hid), 0)
         ends = jnp.where(place == 0, there[0], jnp.where(place == rows + 1, there[1], 1.0))
         ring_col_run = [(-1, -1, self.long, True), (-1, cols, self.long, True)]
@@ -205,7 +206,8 @@
             recv_sem=recv_sem.at[slot, kind, d], device_id=device(d), device_id_type=MESH)
 
     def frame_part(part):
-        return pl.ds(0, 2) if part == 0 else pl.ds(2, steps - 2)
+        first, stop = (0, *PARTS, steps)[part:part + 2]
+        return pl.ds(first, stop - first)
 
     def frame_side(part, d, arriving=False):
         ts = frame_part(part)
@@ -219,13 +221,15 @@
         ts = frame_part(part)
         return pltpu.make_async_copy(frames_ref.at[ts], f_buf.at[ts], f_sem.at[part])
 
+    parts = range(len(PARTS) + 1)
     loads = [(h0_ref, seq_ref.at[steps - 1]), (c0_ref, c_buf), (w_rec_ref, w_buf.at[pl.ds(0, 9 * hid)]), (bias_ref, bias_buf)]
     loads += [(w_in_ref.at[pl.ds(packed * dy, packed)], w_buf.at[pl.ds(9 * hid + LANES * dy, packed)]) for dy in range(3)]
     loads = [pltpu.make_async_copy(src, dst, arg_sem.at[k]) for k, (src, dst) in enumerate(loads)]
     frame_load(0).start()
     for load in loads:
         load.start()
-    frame_load(1).start()
+    for part in parts[1:]:
+        frame_load(part).start()
     for ref in (row_recv, col_recv, corner_recv, crow_recv, ccol_recv, f_side):
         ref[...] = jnp.zeros_like(ref)
     for slot in range(2):
@@ -269,7 +273,6 @@
         c_col[pl.ds(i * rows, rows), :] = c_buf[pl.ds(c, rows, stride=cols), :]
     for i, r in enumerate(edge_rows):
         c_row[pl.ds(i * cols, cols), :] = c_buf[pl.ds(r * cols, cols), :]
-    send_sides(1)
 
     lane = lax.broadcasted_iota(jnp.int32, (1, gates_n), 1)
     scale = jnp.where(lane < 3 * hid, 0.5, 1.0)
@@ -291,7 +294,7 @@
             w_buf[pl.ds(at + packed, 16), :] = bias_rows.astype(BF16)
 
     row = lax.broadcasted_iota(jnp.int32, (LANES - packed, rows), 0)
-    ones = jnp.where(row < 3, 1.0, 0.0).astype(BF16)
+    ones = (row < 3).astype(F32).astype(BF16)
 
     def pack_frame(t, slot):
         for c in range(-1, cols + 1):
@@ -372,7 +375,7 @@
     pack_frame(1, 1)
     stage(0, 0)
     send_halo(0)
-    receive_sides(1)
+    send_sides(1)
 
     def before(m, now):
         t = 2 * m
@@ -391,6 +394,15 @@
         def send():
             stage(1 - now, 2 * (1 - now))
             send_halo(1 - now)
+            if now == 0:
+                @pl.when(m == 0)
+                def _():
+                    receive_sides(1)
+                    send_sides(2)
+
+                @pl.when(m == 2)
+                def _():
+                    receive_sides(2)
 
         before(m, now)
         tile.after_wait(2 * now, send)
@@ -407,7 +419,7 @@
         pair(m, m % 2)
     before(n_pairs - 1, (n_pairs - 1) % 2)
     wait_sent((n_pairs - 1) % 2)
-    for part in (0, 1):
+    for part in parts:
         for d in (2, 3):
             @pl.when(exists(d, n_rows, n_cols))
             def _():
@@ -422,20 +434,25 @@
               for t in range(0, steps - 2, CHUNK)]
     for copy in copies:
         copy.start()
-    tile.after_wait(2 * ((steps // 2 - 1) % 2), lambda: None)
-    for slot in range(2):
-        tile.write_out(1 - slot, out_buf.at[slot])
+    tail = [pltpu.make_async_copy(out_buf.at[k], seq_out.at[steps - 2 + k], sem.at[(steps - 2) // CHUNK + k])
+            for k in range(2)]
+
+    def first_done():
+        tile.write_out(1, out_buf.at[0])
+        tail[0].start()
+
+    tile.after_wait(2 * ((steps // 2 - 1) % 2), first_done)
+    tile.write_out(0, out_buf.at[1])
+    tail[1].start()
     for r in range(2, rows - 2):
         c_buf[pl.ds(r * cols + SIDE, tile.width), :] = c_main[pl.ds((r - 2) * tile.width, tile.width), :]
     for i, c in enumerate(tile.side_cols):
         c_buf[pl.ds(c, rows, stride=cols), :] = c_col[pl.ds(i * rows, rows), :]
     for i, r in enumerate(tile.edge_rows):
         c_buf[pl.ds(r * cols, cols), :] = c_row[pl.ds(i * cols, cols), :]
-    tail = [pltpu.make_async_copy(out_buf, seq_out.at[pl.ds(steps - 2, 2)], sem.at[steps // CHUNK]),
-            pltpu.make_async_copy(c_buf, c_out, sem.at[steps // CHUNK + 1])]
-    for copy in tail:
-        copy.start()
-    for copy in copies + tail:
+    c_copy = pltpu.make_async_copy(c_buf, c_out, sem.at[steps // CHUNK + 1])
+    c_copy.start()
+    for copy in (*copies, *tail, c_copy):
         copy.wait()
 
 
@@ -482,9 +499,9 @@
                     pltpu.VMEM((*both, rows, hid), F32))],
                 pltpu.SemaphoreType.DMA((*both, 8)),
                 pltpu.SemaphoreType.DMA((*both, 8)),
-                pltpu.SemaphoreType.DMA((2,)),
-                pltpu.SemaphoreType.DMA(both),
-                pltpu.SemaphoreType.DMA(both),
+                pltpu.SemaphoreType.DMA((len(PARTS) + 1,)),
+                pltpu.SemaphoreType.DMA((len(PARTS) + 1, 2)),
+                pltpu.SemaphoreType.DMA((len(PARTS) + 1, 2)),
                 pltpu.SemaphoreType.DMA((7,)),
             ],
             compiler_params=pltpu.CompilerParams(

time: 86.8 us -> 85.1 us (0.980)
  Pallas kernels: 85.9 us -> 84.1 us
    pallas_call x1, Pallas kernels: 80.4 us -> 78 us  [local_run(): pl.pallas_call(functools.partial(kernel, sizes), out_shape=(seq_shape, *s...]
where the time goes in v7:
time: 85.1 us; the launch traced here: 84.9 us
  Pallas kernels  84.1 us (99%)
    pallas_call x1, Pallas kernels, local_run(): pl.pallas_call(functools.partial(kernel, sizes), out_shape=(seq_shape, *s...  78 us
    pallas_call x1, Pallas kernels, local_run(): pl.pallas_call(functools.partial(finish_kernel, sizes), out_shape=(seq_sh...  6.17 us

profile of v7, /device:TPU:0, one launch (start us, length us, event | category | flops | bytes accessed | tf_op | source)
XLA Modules:
  0.0 84.9 jit_solution(8907620259523367338)
XLA Ops:
  0.6 78.0 %convlstm.1 = (bf16[24,48,32,128]{3,2,1,0:T(8,128)(2,1)S(1)}, f32[2,2160,128]{2,1,0:T(8,128)S(1)}, f32[4,2160,128]{2,1,0:T(8,128)S(1)}, bf16[1536,512]{1,0:T(8,1...) custom-call(bf16[24,32,16,48]{3,2,1,0:T(8,128)(2,1)} %bitcast.12, ...), custom_call_target="tpu_custom_call" | custom-call | tf_op jit(solution)/shard_map/convlstm/pallas_call | solution.py:484
  78.6 6.2 %finish.1 = (bf16[24,48,32,128]{3,2,1,0:T(8,128)(2,1)}, f32[1536,128]{1,0:T(8,128)}, f32[2,2160,128]{2,1,0:T(8,128)S(1)}, f32[1056,128]{1,0:T(8,128)S(1)}, f32[3...) custom-call(bf16[24,48,32,128]{3,2,1,0:T(8,128)(2,1)S(1)} %get-tuple, ...), custom_call_target="tpu_custom_call", output_to_operand_aliasing={{2}: (1, {}), {3}: (4, {}), {4}: (5, {}), {5}: (6, {})} | custom-call | tf_op jit(solution)/shard_map/finish/pallas_call | solution.py:512

commit v8 on v7

--- a/solution.py
+++ b/solution.py
@@ -17,7 +17,7 @@
 DIRECTIONS = ((-1, 0), (1, 0), (0, -1), (0, 1), (-1, -1), (-1, 1), (1, -1), (1, 1))
 CHUNK = 2
 PARTS = (4, 12)
-FIRST, STOP = 13, 29
+FIRST, STOP = 15, 27
 BLOCK = 11
 SIDE = 4
 
@@ -111,7 +111,7 @@
         for first, stop in ((3, FIRST), (STOP, rows - 11), (rows - 11, rows - 3)):
             self.main_rows(1, pa + 1, first, stop)
 
-    def after_wait(self, pa, send):
+    def after_wait(self, pa, send=lambda: None):
         rows, cols, last = self.rows, self.cols, self.last
         there = [exists(d, self.n_rows, self.n_cols).astype(jnp.int32).astype(F32) for d in range(4)]
         place = lax.broadcasted_iota(jnp.int32, (self.long, self.hid), 0)
@@ -437,13 +437,10 @@
     tail = [pltpu.make_async_copy(out_buf.at[k], seq_out.at[steps - 2 + k], sem.at[(steps - 2) // CHUNK + k])
             for k in range(2)]
 
-    def first_done():
-        tile.write_out(1, out_buf.at[0])
-        tail[0].start()
-
-    tile.after_wait(2 * ((steps // 2 - 1) % 2), first_done)
-    tile.write_out(0, out_buf.at[1])
-    tail[1].start()
+    tile.after_wait(2 * ((steps // 2 - 1) % 2))
+    for k in range(2):
+        tile.write_out(1 - k, out_buf.at[k])
+        tail[k].start()
     for r in range(2, rows - 2):
         c_buf[pl.ds(r * cols + SIDE, tile.width), :] = c_main[pl.ds((r - 2) * tile.width, tile.width), :]
     for i, c in enumerate(tile.side_cols):

time: 85.1 us -> 85.6 us (level)
  no operation moved by 1% of the time
where the time goes in v8:
time: 85.6 us; the launch traced here: 85.4 us
  Pallas kernels  84.6 us (99%)
    pallas_call x1, Pallas kernels, local_run(): pl.pallas_call(functools.partial(kernel, sizes), out_shape=(seq_shape, *s...  78.6 us
    pallas_call x1, Pallas kernels, local_run(): pl.pallas_call(functools.partial(finish_kernel, sizes), out_shape=(seq_sh...  6.03 us

profile of v8, /device:TPU:0, one launch (start us, length us, event | category | flops | bytes accessed | tf_op | source)
XLA Modules:
  0.0 85.4 jit_solution(14710466611320398394)
XLA Ops:
  0.6 78.6 %convlstm.1 = (bf16[24,48,32,128]{3,2,1,0:T(8,128)(2,1)S(1)}, f32[2,2160,128]{2,1,0:T(8,128)S(1)}, f32[4,2160,128]{2,1,0:T(8,128)S(1)}, bf16[1536,512]{1,0:T(8,1...) custom-call(bf16[24,32,16,48]{3,2,1,0:T(8,128)(2,1)} %bitcast.12, ...), custom_call_target="tpu_custom_call" | custom-call | tf_op jit(solution)/shard_map/convlstm/pallas_call | solution.py:481
  79.2 6.0 %finish.1 = (bf16[24,48,32,128]{3,2,1,0:T(8,128)(2,1)}, f32[1536,128]{1,0:T(8,128)}, f32[2,2160,128]{2,1,0:T(8,128)S(1)}, f32[1056,128]{1,0:T(8,128)S(1)}, f32[3...) custom-call(bf16[24,48,32,128]{3,2,1,0:T(8,128)(2,1)S(1)} %get-tuple, ...), custom_call_target="tpu_custom_call", output_to_operand_aliasing={{2}: (1, {}), {3}: (4, {}), {4}: (5, {}), {5}: (6, {})} | custom-call | tf_op jit(solution)/shard_map/finish/pallas_call | solution.py:509

commit v9 on v8

--- a/solution.py
+++ b/solution.py
@@ -17,7 +17,7 @@
 DIRECTIONS = ((-1, 0), (1, 0), (0, -1), (0, 1), (-1, -1), (-1, 1), (1, -1), (1, 1))
 CHUNK = 2
 PARTS = (4, 12)
-FIRST, STOP = 15, 27
+FIRST, STOP = 13, 29
 BLOCK = 11
 SIDE = 4
 
@@ -434,22 +434,20 @@
               for t in range(0, steps - 2, CHUNK)]
     for copy in copies:
         copy.start()
-    tail = [pltpu.make_async_copy(out_buf.at[k], seq_out.at[steps - 2 + k], sem.at[(steps - 2) // CHUNK + k])
-            for k in range(2)]
-
     tile.after_wait(2 * ((steps // 2 - 1) % 2))
-    for k in range(2):
-        tile.write_out(1 - k, out_buf.at[k])
-        tail[k].start()
+    for slot in range(2):
+        tile.write_out(1 - slot, out_buf.at[slot])
     for r in range(2, rows - 2):
         c_buf[pl.ds(r * cols + SIDE, tile.width), :] = c_main[pl.ds((r - 2) * tile.width, tile.width), :]
     for i, c in enumerate(tile.side_cols):
         c_buf[pl.ds(c, rows, stride=cols), :] = c_col[pl.ds(i * rows, rows), :]
     for i, r in enumerate(tile.edge_rows):
         c_buf[pl.ds(r * cols, cols), :] = c_row[pl.ds(i * cols, cols), :]
-    c_copy = pltpu.make_async_copy(c_buf, c_out, sem.at[steps // CHUNK + 1])
-    c_copy.start()
-    for copy in (*copies, *tail, c_copy):
+    tail = [pltpu.make_async_copy(out_buf, seq_out.at[pl.ds(steps - 2, 2)], sem.at[steps // CHUNK]),
+            pltpu.make_async_copy(c_buf, c_out, sem.at[steps // CHUNK + 1])]
+    for copy in tail:
+        copy.start()
+    for copy in copies + tail:
         copy.wait()
 
 

time: 85.6 us -> 84.4 us (0.986)
  Pallas kernels: 84.6 us -> 83.5 us
where the time goes in v9:
time: 84.4 us; the launch traced here: 84.3 us
  Pallas kernels  83.5 us (99%)
    pallas_call x1, Pallas kernels, local_run(): pl.pallas_call(functools.partial(kernel, sizes), out_shape=(seq_shape, *s...  78 us
    pallas_call x1, Pallas kernels, local_run(): pl.pallas_call(functools.partial(finish_kernel, sizes), out_shape=(seq_sh...  5.5 us

profile of v9, /device:TPU:0, one launch (start us, length us, event | category | flops | bytes accessed | tf_op | source)
XLA Modules:
  0.0 84.3 jit_solution(9985974214601111275)
XLA Ops:
  0.6 78.0 %convlstm.1 = (bf16[24,48,32,128]{3,2,1,0:T(8,128)(2,1)S(1)}, f32[2,2160,128]{2,1,0:T(8,128)S(1)}, f32[4,2160,128]{2,1,0:T(8,128)S(1)}, bf16[1536,512]{1,0:T(8,1...) custom-call(bf16[24,32,16,48]{3,2,1,0:T(8,128)(2,1)} %bitcast.12, ...), custom_call_target="tpu_custom_call" | custom-call | tf_op jit(solution)/shard_map/convlstm/pallas_call | solution.py:479
  78.6 5.5 %finish.1 = (bf16[24,48,32,128]{3,2,1,0:T(8,128)(2,1)}, f32[1536,128]{1,0:T(8,128)}, f32[2,2160,128]{2,1,0:T(8,128)S(1)}, f32[1056,128]{1,0:T(8,128)S(1)}, f32[3...) custom-call(bf16[24,48,32,128]{3,2,1,0:T(8,128)(2,1)S(1)} %get-tuple, ...), custom_call_target="tpu_custom_call", output_to_operand_aliasing={{2}: (1, {}), {3}: (4, {}), {4}: (5, {}), {5}: (6, {})} | custom-call | tf_op jit(solution)/shard_map/finish/pallas_call | solution.py:507
